TPU v7x, 32 devices: a whole 2x2x4 slice. The times are simulated.
32 devices in a mesh: tp: 4 (over z), dp: 8 (over y, x, core).
Axes of the slice: x: 2, y: 2, z: 4, core: 2. Of those that a mesh axis runs over, the one named last changes fastest.
Arguments:
- hidden: bfloat16 [8192, 576], P('dp')
- norm_w: bfloat16 [576], replicated
- emb_table: bfloat16 [49152, 576], P('tp')
- teacher: bfloat16 [8192, 49152], P('dp', 'tp')
- loss_mask: int32 [8192], P('dp')
Outputs:
- output 1: float32 [], replicated
- output 2: bfloat16 [8192, 576], P('dp')
- output 3: float32 [49152, 576], P('tp', 'dp')
- output 4: float32 [576], replicated
All inputs are finite; a program needn't handle non-finite values.
Results may differ from a plain program's by a relative error of at most 0.001.
Values sent between devices are 32-bit elements.
A program may use at most 1 GiB of HBM per device.

v0:
```python
import jax
import jax.numpy as jnp
from jax import lax
from jax.sharding import PartitionSpec as P

SOFT_CAP = 30.0
NORM_EPS = 1e-6


def rms_norm(hid_f32, scale_f32):
    inv_rms = lax.rsqrt(jnp.mean(hid_f32 * hid_f32, axis=-1, keepdims=True) + NORM_EPS)
    return hid_f32 * inv_rms * (1.0 + scale_f32)


def solution(mesh):
    def device_fn(hid_loc, norm_w, emb_loc, teach_loc, mask_loc):
        mask_f32 = mask_loc.astype(jnp.float32)
        tok_count = lax.psum(jnp.sum(mask_f32), 'dp')
        weight = mask_f32 / tok_count
        normed_f32, norm_pull = jax.vjp(rms_norm, hid_loc.astype(jnp.float32), norm_w.astype(jnp.float32))
        normed = normed_f32.astype(jnp.bfloat16)
        raw_logit = jnp.einsum('nd,vd->nv', normed, emb_loc, preferred_element_type=jnp.float32)
        tanh_val = jnp.tanh(raw_logit / SOFT_CAP)
        capped = SOFT_CAP * tanh_val
        teach_f32 = teach_loc.astype(jnp.float32)
        maxima = lax.pmax(jnp.stack([jnp.max(capped, axis=-1), jnp.max(teach_f32, axis=-1)], axis=-1), 'tp')
        stu_exp = jnp.exp(capped - maxima[:, 0:1])
        tea_exp = jnp.exp(teach_f32 - maxima[:, 1:2])
        local_sums = jnp.stack([jnp.sum(stu_exp, axis=-1), jnp.sum(tea_exp, axis=-1), jnp.sum(tea_exp * (teach_f32 - capped), axis=-1)], axis=-1)
        totals = lax.psum(local_sums, 'tp')
        lse_stu = maxima[:, 0] + jnp.log(totals[:, 0])
        lse_tea = maxima[:, 1] + jnp.log(totals[:, 1])
        kl_tok = totals[:, 2] / totals[:, 1] - lse_tea + lse_stu
        loss_val = lax.psum(jnp.sum(weight * kl_tok), 'dp')
        prob_diff = stu_exp / totals[:, 0:1] - tea_exp / totals[:, 1:2]
        d_raw = (prob_diff * weight[:, None] * (1.0 - tanh_val * tanh_val)).astype(jnp.bfloat16)
        grad_normed = lax.psum(jnp.dot(d_raw, emb_loc, preferred_element_type=jnp.float32), 'tp')
        emb_part = jnp.einsum('nv,nd->vd', d_raw, normed, preferred_element_type=jnp.float32)
        grad_emb = lax.psum_scatter(emb_part, 'dp', scatter_dimension=1, tiled=True)
        grad_hid, grad_scale = norm_pull(grad_normed)
        grad_w = lax.psum(grad_scale, 'dp')
        return loss_val, grad_hid.astype(jnp.bfloat16), grad_emb, grad_w

    return jax.shard_map(device_fn, mesh=mesh, in_specs=(P('dp', None), P(None), P('tp', None), P('dp', 'tp'), P('dp')), out_specs=(P(), P('dp', None), P('tp', 'dp'), P(None)), check_vma=False)
```

profile of v0, /device:TPU:0, one launch (start us, length us, event | category | flops | bytes accessed | tf_op | source)
XLA Modules:
  0.0 402.7 jit_solution(7776770453929740390)
XLA Ops:
  8.0 0.0 copy-start.4
  8.0 0.0 all-reduce.3.cloned.1.call-start
  8.1 1.4 convert_reduce_fusion
  9.4 15.8 %psum.35 = f32[]{:T(128)} all-reduce(f32[]{:T(128)} %convert_reduce_fusion), channel_id=1, replica_groups=mesh['tp'=4,'dp'=8] {'dp'}, use_global_device_ids=true, to_apply=%region_1.0 | all-reduce | flops 1 | bytes 8 | tf_op jit(solution)/shard_map/psum | solution.py:18
  25.2 13.1 %reduce_max.26 = bf16[1024]{0:T(1024)(128)(2,1)S(1)} reduce(bf16[1024,12288]{1,0:T(8,128)(2,1)} %param.8, bf16[]{:T(256)} %constant.19.clone.1), dimensions={1}, to_apply=%region_4.0 | reduce | flops 12581888 | bytes 25167874 | tf_op jit(solution)/shard_map/reduce_max | solution.py:26
  38.4 0.3 fusion.17
  38.7 0.6 copy-done.1
  39.3 34.9 %fusion.11 = (f32[1024]{0:T(1024)S(1)}, f32[1024,12288]{1,0:T(8,128)}) fusion(bf16[12288,576]{0,1:T(8,128)(2,1)} %param.7, bf16[1024,576]{0,1:T(8,128)(2,1)S(1)} %copy-done, f32[576]{0:T(1024)S(1)} %convert_add_fusion, f32[1024]{0:T(1024)S(1)} %fusion.23), kind=kOutput, calls=%fused_computation.15 | convolution fusion | flops 14535621632 | bytes 65677568 | tf_op jit(solution)/shard_map/nd,vd->nv/dot_general | solution.py:22
  74.2 12.1 %pmax.7 = f32[1024,2]{0,1:T(2,128)S(1)} all-reduce(f32[1024,2]{0,1:T(2,128)S(1)} %pad_maximum_fusion.1), channel_id=1, replica_groups=mesh['tp'=4,'dp'=8] {'tp'}, use_global_device_ids=true, to_apply=%region_5.0 | all-reduce | flops 2048 | bytes 16384 | tf_op jit(solution)/shard_map/pmax | solution.py:26
  86.4 0.0 copy-start.3
  86.4 39.5 %fusion.10 = (f32[1024]{0:T(1024)S(1)}, f32[1024]{0:T(1024)S(1)}, f32[1024]{0:T(1024)S(1)}) fusion(f32[1024,12288]{1,0:T(8,128)} %get-tuple-element.19, f32[1024]{0:T(1024)S(1)} %bitcast.17, f32[1024]{0:T(1024)S(1)} %bitcast.14, bf16[1024,12288]{1,0:T(8,128)(2,1)} %param.8), kind=kLoop, calls=%fused_computation.14 | loop fusion | flops 125826048 | bytes 75517952 | tf_op jit(solution)/shard_map/reduce_sum | solution.py:29
  125.9 15.7 %psum.36 = f32[1024,3]{0,1:T(4,128)S(1)} all-reduce(f32[1024,3]{0,1:T(4,128)S(1)} %pad_maximum_fusion), channel_id=1, replica_groups=mesh['tp'=4,'dp'=8] {'tp'}, use_global_device_ids=true, to_apply=%region_9.0 | all-reduce | flops 3072 | bytes 24576 | tf_op jit(solution)/shard_map/psum | solution.py:30
  141.6 1.3 multiply_reduce_fusion
  142.9 38.8 %fusion.8 = bf16[1024,12288]{1,0:T(8,128)(2,1)} fusion(bf16[1024,12288]{1,0:T(8,128)(2,1)} %param.8, f32[1024,12288]{1,0:T(8,128)} %get-tuple-element.19, f32[1024]{0:T(1024)S(1)} %get-tuple-element.12, f32[1024]{0:T(1024)S(1)} %bitcast.23, f32[1024]{0:T(1024)S(1)} %bitcast.21, f32[1024]{0:T(1024)S(1)} %bitcast.16, f32[1024]{0:T(1024)S(1)} %bitcast.19), kind=kLoop, calls=%fused_computation.12 | loop fusion | flops 163577856 | bytes 100683776 | tf_op jit(solution)/shard_map/convert_element_type | solution.py:36
  181.7 21.4 %fusion.26 = f32[1024,576]{0,1:T(8,128)} fusion(bf16[1024,12288]{1,0:T(8,128)(2,1)} %fusion.8, bf16[12288,576]{0,1:T(8,128)(2,1)} %param.7), kind=kOutput, calls=%fused_computation.41 | convolution fusion | flops 14495514624 | bytes 41680896 | tf_op jit(solution)/shard_map/dot_general | solution.py:37
  203.1 0.0 all-reduce.3.cloned.1.call-update
  203.1 0.0 reduce-scatter.2.cloned.1.call-start
  203.2 25.6 %fusion.19 = f32[12288,576]{0,1:T(8,128)} fusion(bf16[1024,12288]{1,0:T(8,128)(2,1)} %fusion.8, bf16[1024,576]{0,1:T(8,128)(2,1)S(1)} %copy-done, f32[576]{0:T(1024)S(1)} %convert_add_fusion, f32[1024]{0:T(1024)S(1)} %fusion.23), kind=kOutput, calls=%fused_computation.28 | convolution fusion | flops 14497873920 | bytes 54663424 | tf_op jit(solution)/shard_map/nv,nd->vd/dot_general | solution.py:38
  228.8 0.0 reduce-scatter.2.cloned.1.call-update
  228.8 65.1 %all-reduce.3.cloned.1.call-done = f32[1024,576]{0,1:T(8,128)} async-done(((f32[1024,576]{0,1:T(8,128)}), f32[1024,576]{0,1:T(8,128)}) %all-reduce.3.cloned.1.call-update) | async-done | bytes 2359312 | tf_op jit(solution)/shard_map/psum | solution.py:37
  294.0 2.5 fusion.15
  296.4 14.4 %all-reduce = (f32[]{:T(128)}, f32[576]{0:T(1024)}) all-reduce(f32[]{:T(128)} %get-tuple-element.11, f32[576]{0:T(1024)S(1)} %get-tuple-element.7), channel_id=1, replica_groups=mesh['tp'=4,'dp'=8] {'dp'}, use_global_device_ids=true, to_apply=%region_11.0 | all-reduce | flops 577 | bytes 4616 | tf_op jit(solution)/shard_map/psum | solution.py:34
  310.9 3.2 fusion.16
  314.1 81.1 %reduce-scatter.2.cloned.1.call-done = f32[12288,72]{0,1:T(8,128)} async-done(((f32[12288,576]{0,1:T(8,128)}), f32[12288,72]{0,1:T(8,128)}) %reduce-scatter.2.cloned.1.call-update) | async-done | bytes 3538960 | tf_op jit(solution)/shard_map/reduce_scatter | solution.py:39
  (15 shorter events, 0.1 us)
Async XLA Ops:
  8.0 30.4 %copy-start.4 = (bf16[576]{0:T(1024)(128)(2,1)S(1)}, bf16[576]{0:T(1024)(128)(2,1)}, u32[]{:S(2)}) copy-start(bf16[576]{0:T(1024)(128)(2,1)} %param.6) | copy-start | bytes 3460
  8.0 30.4 %copy-start = (bf16[1024,576]{0,1:T(8,128)(2,1)S(1)}, bf16[1024,576]{0,1:T(8,128)(2,1)}, u32[]{:S(2)}) copy-start(bf16[1024,576]{0,1:T(8,128)(2,1)} %param.5) | copy-start | bytes 3538948
  8.0 286.0 %all-reduce.3.cloned.1.call-start = ((), (), s32[]{:S(2)}) async-start(), calls=%async_computation.1 | async-start | bytes 4718592 | tf_op jit(solution)/shard_map/psum | solution.py:37
  38.7 0.6 copy-start.1
  86.4 55.2 %copy-start.3 = (s32[1024]{0:T(1024)S(1)}, s32[1024]{0:T(1024)}, u32[]{:S(2)}) copy-start(s32[1024]{0:T(1024)} %param.9) | copy-start | bytes 12292
  203.1 192.1 %reduce-scatter.2.cloned.1.call-start = ((), (), s32[]{:S(2)}) async-start(), calls=%async_computation.2 | async-start | bytes 31850496 | tf_op jit(solution)/shard_map/reduce_scatter | solution.py:39
  228.8 82.0 %copy-start.2 = (f32[1024]{0:T(1024)S(1)}, f32[1024]{0:T(1024)}, u32[]{:S(2)}) copy-start(f32[1024]{0:T(1024)} %copy-done.1) | copy-start | bytes 12292
Sparse Core Ops, SparseCore 0:
  203.3 90.6 all-reduce.2
Sparse Core Ops, SparseCore 1:
  228.9 166.2 reduce-scatter.1
where the time goes:
time: 403 us
  waiting for transfers between devices  146 us (36%)
  other arithmetic  100 us (25%)
  matrix products  81.9 us (20%)
  blocking collectives  58 us (14%)
  between operations  15.6 us (4%)
    reduce_scatter x1, waiting for transfers between devices, device_fn(): grad_emb = lax.psum_scatter(emb_part, 'dp', scatter_dimension=1, tiled=True)  81.1 us
    psum x1, waiting for transfers between devices, device_fn(): lax.psum(jnp.dot(d_raw, emb_loc, preferred_element_type=jnp.float32), 'tp')  65.1 us
    reduce_sum x1, other arithmetic, device_fn(): jnp.sum(stu_exp, axis=-1)  39.5 us
    convert_element_type x1, other arithmetic, device_fn(): (prob_diff * weight[:, None] * (1.0 - tanh_val * tanh_val)).astype(jnp.bf...  38.8 us
    dot_general x1, matrix products, device_fn(): jnp.einsum('nd,vd->nv', normed, emb_loc, preferred_element_type=jnp.float32)  34.9 us
    dot_general x1, matrix products, device_fn(): jnp.einsum('nv,nd->vd', d_raw, normed, preferred_element_type=jnp.float32)  25.6 us
    dot_general x1, matrix products, device_fn(): jnp.dot(d_raw, emb_loc, preferred_element_type=jnp.float32)  21.4 us
    psum x1, blocking collectives, device_fn(): tok_count = lax.psum(jnp.sum(mask_f32), 'dp')  15.8 us
  transfers between devices with their start and end apart: 2, of which 2 were waited for; matrix products, arithmetic and copies ran while one was open for 8% of the time, Pallas kernels for 0%

commit v1 on v0

v1 whole, which is shorter than its diff:
```python
import jax
import jax.numpy as jnp
from jax import lax
from jax.experimental import pallas as pl
from jax.experimental.pallas import tpu as pltpu
from jax.sharding import PartitionSpec as P

SOFT_CAP = 30.0
NORM_EPS = 1e-6
LOG2E = 1.4426950408889634
LN2 = 0.6931471805599453
CAP2 = SOFT_CAP * LOG2E
D = 576
GRP = 72
TOK = 1024
VLOC = 12288
CW = 512
HALF = CW // 2
NCH = VLOC // CW
RG = 32
F32 = jnp.float32
BF16 = jnp.bfloat16
NT = (((1,), (1,)), ((), ()))


def lane_tiles(arr):
    return [arr[:, k * 128:(k + 1) * 128] for k in range(arr.shape[1] // 128)]


def tree(op, parts):
    while len(parts) > 1:
        parts = [op(parts[k], parts[k + 1]) if k + 1 < len(parts) else parts[k] for k in range(0, len(parts), 2)]
    return parts[0]


def stats_kernel(hid_ref, w_ref, emb_ref, tea_ref, th_ref, gt_ref, st_ref, g_scr, s_acc, m_acc, t_acc):
    step = pl.program_id(0)

    @pl.when(step == 0)
    def _():
        x = hid_ref[...].astype(F32)
        inv = lax.rsqrt(jnp.mean(x * x, axis=0, keepdims=True) + NORM_EPS)
        gn = x * inv * (1.0 + w_ref[...])
        gt_ref[...] = gn.astype(BF16)
        g_scr[...] = jnp.transpose(gn).astype(BF16)
        s_acc[...] = jnp.zeros_like(s_acc)
        t_acc[...] = jnp.zeros_like(t_acc)
        m_acc[...] = jnp.full_like(m_acc, -jnp.inf)

    tb = 256
    for blk in range(TOK // tb):
        raw = jnp.dot(g_scr[blk * tb:(blk + 1) * tb, :], emb_ref[...], preferred_element_type=F32)
        for sub in range(tb // RG):
            rows = slice(blk * tb + sub * RG, blk * tb + (sub + 1) * RG)
            th = jnp.tanh(raw[sub * RG:(sub + 1) * RG, :] * (1.0 / SOFT_CAP))
            th_ref[rows, :] = th
            s_acc[rows, :] += tree(jnp.add, lane_tiles(jnp.exp2(th * CAP2 - CAP2)))
            tea = lane_tiles(tea_ref[rows, :].astype(F32))
            old = m_acc[rows, :]
            new = jnp.maximum(old, tree(jnp.maximum, tea))
            m_acc[rows, :] = new
            t_acc[rows, :] = t_acc[rows, :] * jnp.exp2((old - new) * LOG2E) + tree(
                jnp.add, [jnp.exp2((part - new) * LOG2E) for part in tea])

    @pl.when(step == NCH - 1)
    def _():
        s_row = jnp.sum(jnp.transpose(s_acc[...]), axis=0, keepdims=True)
        m_t = jnp.transpose(m_acc[...])
        m_row = jnp.max(m_t, axis=0, keepdims=True)
        t_row = jnp.sum(jnp.transpose(t_acc[...]) * jnp.exp2((m_t - m_row) * LOG2E), axis=0, keepdims=True)
        st_ref[...] = jnp.concatenate([s_row, m_row, t_row, jnp.zeros((5, TOK), F32)], axis=0)


def first_pass(hid_t, w_col, emb_t, teach):
    return pl.pallas_call(
        stats_kernel,
        grid=(NCH,),
        out_shape=(
            jax.ShapeDtypeStruct((TOK, VLOC), F32),
            jax.ShapeDtypeStruct((D, TOK), BF16),
            jax.ShapeDtypeStruct((8, TOK), F32),
        ),
        in_specs=[
            pl.BlockSpec((D, TOK), lambda i: (0, 0)),
            pl.BlockSpec((D, 1), lambda i: (0, 0)),
            pl.BlockSpec((D, CW), lambda i: (0, i)),
            pl.BlockSpec((TOK, CW), lambda i: (0, i)),
        ],
        out_specs=(
            pl.BlockSpec((TOK, CW), lambda i: (0, i)),
            pl.BlockSpec((D, TOK), lambda i: (0, 0)),
            pl.BlockSpec((8, TOK), lambda i: (0, 0)),
        ),
        scratch_shapes=[pltpu.VMEM((TOK, D), BF16)] + [pltpu.VMEM((TOK, 128), F32)] * 3,
        compiler_params=pltpu.CompilerParams(
            dimension_semantics=("arbitrary",), vmem_limit_bytes=48 * 1024 * 1024),
        cost_estimate=pl.CostEstimate(
            flops=2 * TOK * VLOC * D, bytes_accessed=90_000_000, transcendentals=3 * TOK * VLOC),
    )(hid_t, w_col, emb_t, teach)


def grad_kernel(th_hbm, tea_hbm, emb_hbm, gt_ref, hid_ref, w_ref, st_ref, mask_ref,
                de_ref, dh_ref, dw_ref, loss_ref,
                th_buf, tea_buf, emb_buf, dr0, dr1, pp0, pp1, r1, r2a, r2b, r3a, r3b,
                dg_ref, ar_in, dh_f, st_in, cnt_in, cnt_own, wgt, l2s, mtx, l2t, kl_acc,
                in_sem, st_send, st_recv, cnt_send, cnt_recv,
                s1_send, s1_recv, s2_send, s2_recv, s3_send, s3_recv,
                ar_send, ar_recv, bc_send, bc_recv):
    z = lax.axis_index('tp')
    d = lax.axis_index('dp')
    core = d % 2
    xx = (d // 2) % 2
    yy = d // 4
    partner = d + 1 - 2 * core
    xnbr = d + 2 - 4 * xx
    ynbr = d + 4 - 8 * yy

    def fetch(i):
        cols = pl.ds(pl.multiple_of(i * CW, CW), CW)
        three = i % 3
        four = i % 4
        return (
            pltpu.make_async_copy(th_hbm.at[:, cols], th_buf.at[three], in_sem.at[0, three]),
            pltpu.make_async_copy(tea_hbm.at[:, cols], tea_buf.at[three], in_sem.at[1, three]),
            pltpu.make_async_copy(emb_hbm.at[:, cols], emb_buf.at[four], in_sem.at[2, four]),
        )

    def start_fetch(i):
        for cp in fetch(i):
            cp.start()

    start_fetch(0)
    start_fetch(1)

    barrier = pltpu.get_barrier_semaphore()
    for k in range(1, 4):
        pl.semaphore_signal(barrier, inc=1, device_id={'tp': (z + k) % 4})
    for k in range(1, 8):
        pl.semaphore_signal(barrier, inc=1, device_id={'dp': (d + k) % 8})
    cnt_own[...] = jnp.full((8, 128), jnp.sum(mask_ref[...]), F32)
    pl.semaphore_wait(barrier, 10)

    def st_copy(k):
        return pltpu.make_async_remote_copy(
            src_ref=st_ref, dst_ref=st_in.at[k], send_sem=st_send.at[k], recv_sem=st_recv.at[k],
            device_id={'tp': (z + k) % 4})

    def cnt_copy(k):
        return pltpu.make_async_remote_copy(
            src_ref=cnt_own, dst_ref=cnt_in.at[k], send_sem=cnt_send.at[k], recv_sem=cnt_recv.at[k],
            device_id={'dp': (d + k) % 8})

    for k in range(1, 4):
        st_copy(k).start()
    for k in range(1, 8):
        cnt_copy(k).start()
    dg_ref[...] = jnp.zeros_like(dg_ref)
    kl_acc[...] = jnp.zeros_like(kl_acc)
    dw_ref[...] = jnp.zeros_like(dw_ref)
    for k in range(1, 4):
        st_copy(k).wait_recv()
    for k in range(1, 8):
        cnt_copy(k).wait_recv()

    stats = [st_ref[...]] + [st_in[k] for k in range(1, 4)]
    s_tot = tree(jnp.add, [st[0:1, :] for st in stats])
    m_tot = tree(jnp.maximum, [st[1:2, :] for st in stats])
    t_tot = tree(jnp.add, [st[2:3, :] * jnp.exp2((st[1:2, :] - m_tot) * LOG2E) for st in stats])
    count = cnt_own[0:1, :]
    for k in range(1, 8):
        count = count + cnt_in[k][0:1, :]
    w_row = mask_ref[...] / jnp.concatenate([count] * (TOK // 128), axis=1)
    l2s_row = jnp.log2(s_tot) + CAP2
    l2t_row = jnp.log2(t_tot)

    def to_rows(row):
        return jnp.transpose(jnp.broadcast_to(row, (128, TOK)))

    wgt[...] = to_rows(w_row)
    l2s[...] = to_rows(l2s_row)
    mtx[...] = to_rows(m_tot)
    l2t[...] = to_rows(l2t_row)
    lse_part = w_row * ((l2s_row - l2t_row) * LN2 - m_tot)
    lse_sum = jnp.where(z == 0, jnp.sum(lse_part), 0.0)

    def elementwise(i, dr_ref, lo, hi):
        slot = i % 3
        for sub in range(lo, hi):
            rows = slice(sub * RG, (sub + 1) * RG)
            w_b, ls_b, m_b, lt_b = wgt[rows, :], l2s[rows, :], mtx[rows, :], l2t[rows, :]
            kl = []
            for q in range(CW // 128):
                cols = slice(q * 128, (q + 1) * 128)
                th = th_buf[slot, rows, cols]
                tea = tea_buf[slot, rows, cols].astype(F32)
                p_s = jnp.exp2(th * CAP2 - ls_b)
                p_t = jnp.exp2((tea - m_b) * LOG2E - lt_b)
                kl.append(p_t * (tea - SOFT_CAP * th))
                dr_ref[rows, cols] = ((p_s - p_t) * w_b * (1.0 - th * th)).astype(BF16)
            kl_acc[rows, :] += tree(jnp.add, kl)

    def emb_piece(dr_ref, pp_ref, k):
        part = jnp.dot(gt_ref[...], dr_ref[:, k * HALF:(k + 1) * HALF], preferred_element_type=F32)
        for grp in range(8):
            pp_ref[grp % 2, grp // 4, (grp // 2) % 2, :, k * HALF:(k + 1) * HALF] = part[grp * GRP:(grp + 1) * GRP, :]

    def hid_piece(i, dr_ref, k):
        cols = slice(k * 256, (k + 1) * 256)
        dg_ref[:, cols] += lax.dot_general(emb_buf[i % 4], dr_ref[cols, :], NT, preferred_element_type=F32)

    def s1_copy(c, pp_ref):
        return pltpu.make_async_remote_copy(
            src_ref=pp_ref.at[1 - core], dst_ref=r1.at[c], send_sem=s1_send.at[c], recv_sem=s1_recv.at[c],
            device_id={'dp': partner})

    def s2_copies(c):
        return (
            pltpu.make_async_remote_copy(
                src_ref=r1.at[c, :, 1 - xx, :, pl.ds(0, HALF)], dst_ref=r2a.at[c],
                send_sem=s2_send.at[0, c], recv_sem=s2_recv.at[0, c], device_id={'dp': xnbr}),
            pltpu.make_async_remote_copy(
                src_ref=r1.at[c, 1 - yy, :, :, pl.ds(HALF, HALF)], dst_ref=r2b.at[c],
                send_sem=s2_send.at[1, c], recv_sem=s2_recv.at[1, c], device_id={'dp': ynbr}),
        )

    def s3_copies(c):
        return (
            pltpu.make_async_remote_copy(
                src_ref=r2a.at[c, 1 - yy], dst_ref=r3a.at[c],
                send_sem=s3_send.at[0, c], recv_sem=s3_recv.at[0, c], device_id={'dp': ynbr}),
            pltpu.make_async_remote_copy(
                src_ref=r2b.at[c, 1 - xx], dst_ref=r3b.at[c],
                send_sem=s3_send.at[1, c], recv_sem=s3_recv.at[1, c], device_id={'dp': xnbr}),
        )

    def stage2(c, pp_ref):
        s1_copy(c, pp_ref).wait_recv()
        for q in range(4):
            r1[c, q // 2, q % 2] += pp_ref[core, q // 2, q % 2]
        for cp in s2_copies(c):
            cp.start()

    def stage3(c):
        first, second = s2_copies(c)
        first.wait_recv()
        for q in range(2):
            r2a[c, q] += r1[c, q, xx, :, 0:HALF]
        second.wait_recv()
        for q in range(2):
            r2b[c, q] += r1[c, yy, q, :, HALF:CW]
        for cp in s3_copies(c):
            cp.start()

    def stage4(c):
        first, second = s3_copies(c)
        base = pl.multiple_of(c * CW, CW)
        first.wait_recv()
        de_ref[:, pl.ds(base, HALF)] = r2a[c, yy] + r3a[c]
        second.wait_recv()
        de_ref[:, pl.ds(pl.multiple_of(base + HALF, HALF), HALF)] = r2b[c, xx] + r3b[c]

    nsub = TOK // RG

    def wait_in(i):
        for cp in fetch(i):
            cp.wait()

    def both(i, dr_new, dr_old, pp_ref, cuts=6):
        for k in range(cuts):
            if k < 2:
                emb_piece(dr_old, pp_ref, k)
            else:
                hid_piece(i - 1, dr_old, k - 2)
            elementwise(i, dr_new, nsub * k // cuts, nsub * (k + 1) // cuts)

    wait_in(0)
    start_fetch(2)
    elementwise(0, dr0, 0, nsub)
    wait_in(1)
    start_fetch(3)
    both(1, dr1, dr0, pp0)
    s1_copy(0, pp0).start()

    def pair(t, carry):
        for par, (dr_new, dr_old, pp_new, pp_old) in enumerate(((dr0, dr1, pp1, pp0), (dr1, dr0, pp0, pp1))):
            i = 2 + 2 * t + par
            wait_in(i)

            @pl.when(i + 2 < NCH)
            def _():
                start_fetch(i + 2)

            @pl.when(i >= 3)
            def _():
                s1_copy(i - 3, pp_new).wait_send()

            both(i, dr_new, dr_old, pp_new)
            s1_copy(i - 1, pp_new).start()
            stage2(i - 2, pp_old)
        return carry

    lax.fori_loop(0, (NCH - 2) // 2, pair, 0)
    s1_copy(NCH - 3, pp1).wait_send()
    for k in range(2):
        emb_piece(dr1, pp1, k)
    s1_copy(NCH - 1, pp1).start()
    for k in range(4):
        hid_piece(NCH - 1, dr1, k)

    def where_of(h):
        pos = z if h == 0 else 3 - z
        up = z + 1 if h == 0 else z - 1
        down = z - 1 if h == 0 else z + 1
        return pos, up, down

    def lanes(h, b):
        lo = h * 512 + b * 128
        return slice(lo, lo + 128)

    def ar_first(h, b):
        pos, up, _ = where_of(h)
        idx = 4 * h + b
        return pltpu.make_async_remote_copy(
            src_ref=dg_ref.at[:, pl.ds(h * 512 + b * 128, 128)], dst_ref=ar_in.at[idx],
            send_sem=ar_send.at[idx], recv_sem=ar_recv.at[idx], device_id={'tp': up})

    def ar_next(h, b):
        pos, up, _ = where_of(h)
        idx = 4 * h + b
        return pltpu.make_async_remote_copy(
            src_ref=ar_in.at[idx], dst_ref=ar_in.at[idx],
            send_sem=ar_send.at[idx], recv_sem=ar_recv.at[idx], device_id={'tp': up})

    def bc_copy(h, b):
        _, _, down = where_of(h)
        idx = 4 * h + b
        part = dh_f.at[:, pl.ds(h * 512 + b * 128, 128)]
        return pltpu.make_async_remote_copy(
            src_ref=part, dst_ref=part,
            send_sem=bc_send.at[idx], recv_sem=bc_recv.at[idx], device_id={'tp': down})

    for b in range(4):
        for h in range(2):
            @pl.when(where_of(h)[0] == 0)
            def _():
                ar_first(h, b).start()

    def reduce_step(h, b):
        pos, _, _ = where_of(h)
        idx = 4 * h + b

        @pl.when(pos > 0)
        def _():
            ar_next(h, b).wait_recv()

            @pl.when(pos < 3)
            def _():
                ar_in[idx] += dg_ref[:, lanes(h, b)]
                ar_next(h, b).start()

            @pl.when(pos == 3)
            def _():
                dg = ar_in[idx] + dg_ref[:, lanes(h, b)]
                x = hid_ref[:, lanes(h, b)].astype(F32)
                inv = lax.rsqrt(jnp.mean(x * x, axis=0, keepdims=True) + NORM_EPS)
                dw_ref[...] += dg * (x * inv)
                du = dg * (1.0 + w_ref[...])
                inner = jnp.sum(du * x, axis=0, keepdims=True)
                dh_f[:, lanes(h, b)] = du * inv - x * (inv * inv * inv * inner * (1.0 / D))
                bc_copy(h, b).start()

    def spread_step(h, b):
        pos, _, _ = where_of(h)

        @pl.when(pos < 3)
        def _():
            bc_copy(h, b).wait_recv()

            @pl.when(pos > 0)
            def _():
                bc_copy(h, b).start()

        dh_ref[:, lanes(h, b)] = dh_f[:, lanes(h, b)].astype(BF16)

    stage2(NCH - 2, pp0)
    stage2(NCH - 1, pp1)

    def loop(lo, hi, fn):
        def body(c, carry):
            fn(c)
            return carry
        lax.fori_loop(lo, hi, body, 0)

    loop(0, 8, stage3)
    for b in range(4):
        reduce_step(0, b)
        reduce_step(1, b)
        loop(8 + 4 * b, 12 + 4 * b, stage3)
    for b in range(4):
        spread_step(0, b)
        spread_step(1, b)
        loop(6 * b, 6 * b + 6, stage4)

    def wsum(k, carry):
        rows = pl.ds(pl.multiple_of(k * 8, 8), 8)
        return carry + wgt[rows, :] * kl_acc[rows, :]

    kl_tile = lax.fori_loop(0, TOK // 8, wsum, jnp.zeros((8, 128), F32))
    loss_ref[...] = kl_tile + lse_sum * (1.0 / 1024.0)

    for k in range(1, 4):
        st_copy(k).wait_send()
    for k in range(1, 8):
        cnt_copy(k).wait_send()
    s1_copy(NCH - 2, pp0).wait_send()
    s1_copy(NCH - 1, pp1).wait_send()

    def drain(c):
        for cp in s2_copies(c) + s3_copies(c):
            cp.wait_send()

    loop(0, NCH, drain)
    for h in range(2):
        pos = where_of(h)[0]
        for b in range(4):
            @pl.when(pos < 3)
            def _():
                ar_next(h, b).wait_send()

            @pl.when(pos > 0)
            def _():
                bc_copy(h, b).wait_send()


def second_pass(th, teach, emb_t, g_t, hid_t, w_col, stats, mask_row):
    vmem = pl.BlockSpec(memory_space=pltpu.VMEM)
    hbm = pl.BlockSpec(memory_space=pl.ANY)
    dma = pltpu.SemaphoreType.DMA
    return pl.pallas_call(
        grad_kernel,
        out_shape=(
            jax.ShapeDtypeStruct((GRP, VLOC), F32),
            jax.ShapeDtypeStruct((D, TOK), BF16),
            jax.ShapeDtypeStruct((D, 128), F32),
            jax.ShapeDtypeStruct((8, 128), F32),
        ),
        in_specs=[hbm] * 3 + [vmem] * 5,
        out_specs=(vmem,) * 4,
        scratch_shapes=[
            pltpu.VMEM((3, TOK, CW), F32),
            pltpu.VMEM((3, TOK, CW), BF16),
            pltpu.VMEM((4, D, CW), BF16),
            pltpu.VMEM((TOK, CW), BF16),
            pltpu.VMEM((TOK, CW), BF16),
            pltpu.VMEM((2, 2, 2, GRP, CW), F32),
            pltpu.VMEM((2, 2, 2, GRP, CW), F32),
            pltpu.VMEM((NCH, 2, 2, GRP, CW), F32),
            pltpu.VMEM((NCH, 2, GRP, HALF), F32),
            pltpu.VMEM((NCH, 2, GRP, HALF), F32),
            pltpu.VMEM((NCH, GRP, HALF), F32),
            pltpu.VMEM((NCH, GRP, HALF), F32),
            pltpu.VMEM((D, TOK), F32),
            pltpu.VMEM((8, D, 128), F32),
            pltpu.VMEM((D, TOK), F32),
            pltpu.VMEM((4, 8, TOK), F32),
            pltpu.VMEM((8, 8, 128), F32),
            pltpu.VMEM((8, 128), F32),
        ] + [pltpu.VMEM((TOK, 128), F32)] * 5 + [
            dma((3, 4)), dma((4,)), dma((4,)), dma((8,)), dma((8,)),
            dma((NCH,)), dma((NCH,)), dma((2, NCH)), dma((2, NCH)), dma((2, NCH)), dma((2, NCH)),
            dma((8,)), dma((8,)), dma((8,)), dma((8,)),
        ],
        compiler_params=pltpu.CompilerParams(
            collective_id=0, has_side_effects=True, vmem_limit_bytes=67_000_000),
        cost_estimate=pl.CostEstimate(
            flops=4 * TOK * VLOC * D, bytes_accessed=100_000_000, transcendentals=2 * TOK * VLOC),
    )(th, teach, emb_t, g_t, hid_t, w_col, stats, mask_row)


def solution(mesh):
    def device_fn(hid_loc, norm_w, emb_loc, teach_loc, mask_loc):
        hid_t = hid_loc.T
        emb_t = emb_loc.T
        w_col = norm_w.astype(F32).reshape(D, 1)
        mask_row = mask_loc.astype(F32).reshape(1, TOK)
        th, g_t, stats = first_pass(hid_t, w_col, emb_t, teach_loc)
        de_t, dh_t, dw_part, loss_part = second_pass(th, teach_loc, emb_t, g_t, hid_t, w_col, stats, mask_row)
        packed = jnp.concatenate([jnp.sum(dw_part, axis=1), jnp.sum(loss_part).reshape(1)])
        total = lax.psum(packed, ('tp', 'dp'))
        return total[D], dh_t.T, de_t.T, total[:D]

    return jax.shard_map(device_fn, mesh=mesh, in_specs=(P('dp', None), P(None), P('tp', None), P('dp', 'tp'), P('dp')), out_specs=(P(), P('dp', None), P('tp', 'dp'), P(None)), check_vma=False)
```

time: 403 us -> 299 us (0.74)
  Pallas kernels: 0 us -> 239 us
  waiting for transfers between devices: 146 us -> 0 us
  other arithmetic: 100 us -> 4.42 us
  matrix products: 81.9 us -> 0 us
  blocking collectives: 58 us -> 42.9 us
  between operations: 15.6 us -> 0.66 us
  local copies, waits for them, and re-layouts: 0.63 us -> 10.7 us
    pallas_call x0 -> x2, Pallas kernels: none -> 239 us  [the longest x1 192 us: second_pass(): pl.pallas_call(grad_kernel, out_shape=(jax.ShapeDtypeStruct((GRP, VLOC),...]
    dot_general x3 -> x0, matrix products: 81.9 us -> none  [the longest x1 34.9 us: device_fn(): jnp.einsum('nd,vd->nv', normed, emb_loc, preferred_element_type=jnp.float32)]
    reduce_scatter x1 -> x0, waiting for transfers between devices: 81.1 us -> none  [device_fn(): grad_emb = lax.psum_scatter(emb_part, 'dp', scatter_dimension=1, tiled=True)]
    psum x1 -> x0, waiting for transfers between devices: 65.1 us -> none  [device_fn(): lax.psum(jnp.dot(d_raw, emb_loc, preferred_element_type=jnp.float32), 'tp')]
    reduce_sum x5 -> x2, other arithmetic: 44.9 us -> 2.41 us  [the longest x1 1.28 us: device_fn(): jnp.sum(loss_part).reshape(1)]
    convert_element_type x2 -> x1, other arithmetic: 42 us -> 1.28 us  [device_fn(): mask_row = mask_loc.astype(F32).reshape(1, TOK)]
    reduce_max x2 -> x0, other arithmetic: 13.1 us -> none  [device_fn(): jnp.max(teach_f32, axis=-1)]
    pmax x1 -> x0, blocking collectives: 12.1 us -> none  [device_fn(): lax.pmax(jnp.stack([jnp.max(capped, axis=-1), jnp.max(teach_f32, axis=-1)...]
  transfers between devices with their start and end apart: 2 -> 0, of which waited for: 2 -> 0; matrix products, arithmetic and copies ran while one was open for 8% -> 0% of each run, Pallas kernels for 0% -> 0%
where the time goes in v1:
time: 299 us; the launch traced here: 298 us
  Pallas kernels  239 us (80%)
  blocking collectives  42.9 us (14%)
  local copies, waits for them, and re-layouts  10.7 us (4%)
  other arithmetic  4.42 us (1%)
    pallas_call x1, Pallas kernels, second_pass(): pl.pallas_call(grad_kernel, out_shape=(jax.ShapeDtypeStruct((GRP, VLOC),...  192 us
    pallas_call x1, Pallas kernels, first_pass(): pl.pallas_call(stats_kernel, grid=(NCH,), out_shape=(jax.ShapeDtypeStruct...  47 us
    psum x1, blocking collectives, device_fn(): total = lax.psum(packed, ('tp', 'dp'))  42.9 us
    unnamed x12, local copies, waits for them, and re-layouts  9.28 us

profile of v1, /device:TPU:0, one launch (start us, length us, event | category | flops | bytes accessed | tf_op | source)
XLA Modules:
  0.0 297.7 jit_solution(3834981359831312089)
XLA Ops:
  0.6 1.3 convert_element_type.4
  1.9 0.8 reshape.25.w_ref
  2.7 0.0 copy-start.1
  2.7 1.3 copy-done.1
  4.0 0.0 copy-start
  4.0 47.0 %shard_map.84 = (f32[1024,12288]{1,0:T(8,128)}, bf16[576,1024]{1,0:T(8,128)(2,1)S(1)}, f32[8,1024]{1,0:T(8,128)S(1)}) custom-call(bf16[576,1024]{1,0:T(8,128)(2,1)S(1)} %bitcast.9, f32[576,1]{1,0:T(8,128)S(1)} %reshape.25.w_ref, bf16[576,12288]{1,0:T(8,128)(2,1)} %bitcast.14, bf16[1024,12288]{1,0:T(8,128)(2,1)} %tea_hbm.1), custom_call_target="tpu_custom_call" | custom-call | flops 14495514624 | bytes 90000000 | tf_op jit(solution)/shard_map/pallas_call | solution.py:75
  51.0 0.0 copy-done
  51.0 0.0 copy-start.2
  51.0 1.0 copy-done.2
  52.0 0.0 copy-start.3
  52.0 0.6 copy-done.3
  52.6 192.0 %shard_map.85 = (f32[72,12288]{1,0:T(8,128)}, bf16[576,1024]{1,0:T(8,128)(2,1)}, f32[576,128]{1,0:T(8,128)}, f32[8,128]{1,0:T(8,128)}) custom-call(f32[1024,12288]{1,0:T(8,128)} %get-tuple-element.11.th_hbm, bf16[1024,12288]{1,0:T(8,128)(2,1)} %tea_hbm.1, bf16[576,12288]{1,0:T(8,128)(2,1)} %bitcast.15, bf16[576,1024]{1,0:T(8,128)(2,1)} %copy-done.2, ...), custom_call_target="tpu_custom_call" | custom-call | flops 28991029248 | bytes 100000000 | tf_op jit(solution)/shard_map/pallas_call | solution.py:439
  244.7 1.3 reduce_sum.19
  246.0 1.1 reduce_sum.18
  247.1 0.7 pad_maximum_fusion
  247.8 42.9 %psum.7 = f32[577]{0:T(1024)S(1)} all-reduce(f32[577]{0:T(1024)S(1)} %pad_maximum_fusion), channel_id=1, replica_groups=mesh['tp'=4,'dp'=8] {'tp','dp'}, use_global_device_ids=true, to_apply=%region_2.0 | all-reduce | flops 577 | bytes 4616 | tf_op jit(solution)/shard_map/psum | solution.py:489
  290.7 0.0 copy-start.4
  290.7 0.6 slice.6
  291.3 2.4 copy.13
  293.7 4.0 %copy.14 = f32[12288,72]{0,1:T(8,128)} copy(f32[12288,72]{0,1:T(8,128)} %bitcast.10) | data formatting | bytes 7077888
  297.7 0.0 copy-done.4
Async XLA Ops:
  2.7 1.3 copy-start.1
  4.0 47.0 %copy-start = (f32[576,1]{1,0:T(8,128)}, f32[576,1]{1,0:T(8,128)S(1)}, u32[]{:S(2)}) copy-start(f32[576,1]{1,0:T(8,128)S(1)} %reshape.25.w_ref) | copy-start | bytes 6916
  51.0 1.0 copy-start.2
  52.0 0.6 copy-start.3
  290.7 7.0 %copy-start.4 = (f32[577]{0:T(1024)}, f32[577]{0:T(1024)S(1)}, u32[]{:S(2)}) copy-start(f32[577]{0:T(1024)S(1)} %psum.7) | copy-start | bytes 6928

commit v2 on v1

--- a/solution.py
+++ b/solution.py
@@ -17,6 +17,8 @@
 CW = 512
 HALF = CW // 2
 NCH = VLOC // CW
+CWA = 512
+NCHA = VLOC // CWA
 RG = 32
 F32 = jnp.float32
 BF16 = jnp.bfloat16
@@ -62,7 +64,7 @@
             t_acc[rows, :] = t_acc[rows, :] * jnp.exp2((old - new) * LOG2E) + tree(
                 jnp.add, [jnp.exp2((part - new) * LOG2E) for part in tea])
 
-    @pl.when(step == NCH - 1)
+    @pl.when(step == NCHA - 1)
     def _():
         s_row = jnp.sum(jnp.transpose(s_acc[...]), axis=0, keepdims=True)
         m_t = jnp.transpose(m_acc[...])
@@ -74,7 +76,7 @@
 def first_pass(hid_t, w_col, emb_t, teach):
     return pl.pallas_call(
         stats_kernel,
-        grid=(NCH,),
+        grid=(NCHA,),
         out_shape=(
             jax.ShapeDtypeStruct((TOK, VLOC), F32),
             jax.ShapeDtypeStruct((D, TOK), BF16),
@@ -83,11 +85,11 @@
         in_specs=[
             pl.BlockSpec((D, TOK), lambda i: (0, 0)),
             pl.BlockSpec((D, 1), lambda i: (0, 0)),
-            pl.BlockSpec((D, CW), lambda i: (0, i)),
-            pl.BlockSpec((TOK, CW), lambda i: (0, i)),
+            pl.BlockSpec((D, CWA), lambda i: (0, i)),
+            pl.BlockSpec((TOK, CWA), lambda i: (0, i)),
         ],
         out_specs=(
-            pl.BlockSpec((TOK, CW), lambda i: (0, i)),
+            pl.BlockSpec((TOK, CWA), lambda i: (0, i)),
             pl.BlockSpec((D, TOK), lambda i: (0, 0)),
             pl.BlockSpec((8, TOK), lambda i: (0, 0)),
         ),
@@ -100,12 +102,12 @@
 
 
 def grad_kernel(th_hbm, tea_hbm, emb_hbm, gt_ref, hid_ref, w_ref, st_ref, mask_ref,
-                de_ref, dh_ref, dw_ref, loss_ref,
+                de_ref, dh_ref, small_ref,
                 th_buf, tea_buf, emb_buf, dr0, dr1, pp0, pp1, r1, r2a, r2b, r3a, r3b,
-                dg_ref, ar_in, dh_f, st_in, cnt_in, cnt_own, wgt, l2s, mtx, l2t, kl_acc,
+                dg_ref, ar_in, dh_f, st_in, cnt_in, cnt_own, dw_acc, sm_dp, sm_tp, wgt, l2s, mtx, l2t, kl_acc,
                 in_sem, st_send, st_recv, cnt_send, cnt_recv,
                 s1_send, s1_recv, s2_send, s2_recv, s3_send, s3_recv,
-                ar_send, ar_recv, bc_send, bc_recv):
+                ar_send, ar_recv, bc_send, bc_recv, smd_send, smd_recv, smt_send, smt_recv):
     z = lax.axis_index('tp')
     d = lax.axis_index('dp')
     core = d % 2
@@ -156,7 +158,7 @@
         cnt_copy(k).start()
     dg_ref[...] = jnp.zeros_like(dg_ref)
     kl_acc[...] = jnp.zeros_like(kl_acc)
-    dw_ref[...] = jnp.zeros_like(dw_ref)
+    dw_acc[...] = jnp.zeros_like(dw_acc)
     for k in range(1, 4):
         st_copy(k).wait_recv()
     for k in range(1, 8):
@@ -233,10 +235,12 @@
                 send_sem=s3_send.at[1, c], recv_sem=s3_recv.at[1, c], device_id={'dp': xnbr}),
         )
 
-    def stage2(c, pp_ref):
+    def stage1(c, pp_ref):
         s1_copy(c, pp_ref).wait_recv()
         for q in range(4):
             r1[c, q // 2, q % 2] += pp_ref[core, q // 2, q % 2]
+
+    def stage2(c):
         for cp in s2_copies(c):
             cp.start()
 
@@ -281,6 +285,14 @@
     both(1, dr1, dr0, pp0)
     s1_copy(0, pp0).start()
 
+    def tick(t):
+        stage2(t + 1)
+        stage3(t - 1)
+
+        @pl.when(t >= 3)
+        def _():
+            stage4(t - 3)
+
     def pair(t, carry):
         for par, (dr_new, dr_old, pp_new, pp_old) in enumerate(((dr0, dr1, pp1, pp0), (dr1, dr0, pp0, pp1))):
             i = 2 + 2 * t + par
@@ -296,10 +308,23 @@
 
             both(i, dr_new, dr_old, pp_new)
             s1_copy(i - 1, pp_new).start()
-            stage2(i - 2, pp_old)
+            stage1(i - 2, pp_old)
+            if par == 0:
+                @pl.when(t == 0)
+                def _():
+                    stage2(0)
+
+                @pl.when(t > 0)
+                def _():
+                    tick(t)
+            else:
+                @pl.when(t == 0)
+                def _():
+                    stage2(1)
         return carry
 
-    lax.fori_loop(0, (NCH - 2) // 2, pair, 0)
+    npair = (NCH - 2) // 2
+    lax.fori_loop(0, npair, pair, 0)
     s1_copy(NCH - 3, pp1).wait_send()
     for k in range(2):
         emb_piece(dr1, pp1, k)
@@ -345,68 +370,125 @@
             def _():
                 ar_first(h, b).start()
 
-    def reduce_step(h, b):
-        pos, _, _ = where_of(h)
+    def add_on(h, b):
         idx = 4 * h + b
-
-        @pl.when(pos > 0)
-        def _():
-            ar_next(h, b).wait_recv()
-
-            @pl.when(pos < 3)
-            def _():
-                ar_in[idx] += dg_ref[:, lanes(h, b)]
-                ar_next(h, b).start()
-
-            @pl.when(pos == 3)
-            def _():
-                dg = ar_in[idx] + dg_ref[:, lanes(h, b)]
-                x = hid_ref[:, lanes(h, b)].astype(F32)
-                inv = lax.rsqrt(jnp.mean(x * x, axis=0, keepdims=True) + NORM_EPS)
-                dw_ref[...] += dg * (x * inv)
-                du = dg * (1.0 + w_ref[...])
-                inner = jnp.sum(du * x, axis=0, keepdims=True)
-                dh_f[:, lanes(h, b)] = du * inv - x * (inv * inv * inv * inner * (1.0 / D))
-                bc_copy(h, b).start()
-
-    def spread_step(h, b):
-        pos, _, _ = where_of(h)
-
-        @pl.when(pos < 3)
-        def _():
-            bc_copy(h, b).wait_recv()
-
-            @pl.when(pos > 0)
-            def _():
-                bc_copy(h, b).start()
-
-        dh_ref[:, lanes(h, b)] = dh_f[:, lanes(h, b)].astype(BF16)
-
-    stage2(NCH - 2, pp0)
-    stage2(NCH - 1, pp1)
-
-    def loop(lo, hi, fn):
-        def body(c, carry):
-            fn(c)
-            return carry
-        lax.fori_loop(lo, hi, body, 0)
-
-    loop(0, 8, stage3)
-    for b in range(4):
-        reduce_step(0, b)
-        reduce_step(1, b)
-        loop(8 + 4 * b, 12 + 4 * b, stage3)
-    for b in range(4):
-        spread_step(0, b)
-        spread_step(1, b)
-        loop(6 * b, 6 * b + 6, stage4)
+        ar_next(h, b).wait_recv()
+        ar_in[idx] += dg_ref[:, lanes(h, b)]
+        ar_next(h, b).start()
+
+    def finish(h, b):
+        ar_next(h, b).wait_recv()
+        dg = ar_in[4 * h + b] + dg_ref[:, lanes(h, b)]
+        x = hid_ref[:, lanes(h, b)].astype(F32)
+        inv = lax.rsqrt(jnp.mean(x * x, axis=0, keepdims=True) + NORM_EPS)
+        dw_acc[...] += dg * (x * inv)
+        du = dg * (1.0 + w_ref[...])
+        inner = jnp.sum(du * x, axis=0, keepdims=True)
+        dh_f[:, lanes(h, b)] = du * inv - x * (inv * inv * inv * inner * (1.0 / D))
+        bc_copy(h, b).start()
+
+    def spread(h, b, pos):
+        bc_copy(h, b).wait_recv()
+        if pos > 0:
+            bc_copy(h, b).start()
+
+    def slot(s):
+        for pos in (1, 2, 3):
+            b = s - (pos - 1)
+            if 0 <= b < 4:
+                for h in range(2):
+                    @pl.when(where_of(h)[0] == pos)
+                    def _():
+                        if pos < 3:
+                            add_on(h, b)
+                        else:
+                            finish(h, b)
+        for pos in (2, 1, 0):
+            b = s - 4 - (2 - pos)
+            if 0 <= b < 4:
+                for h in range(2):
+                    @pl.when(where_of(h)[0] == pos)
+                    def _():
+                        spread(h, b, pos)
 
     def wsum(k, carry):
         rows = pl.ds(pl.multiple_of(k * 8, 8), 8)
         return carry + wgt[rows, :] * kl_acc[rows, :]
 
-    kl_tile = lax.fori_loop(0, TOK // 8, wsum, jnp.zeros((8, 128), F32))
-    loss_ref[...] = kl_tile + lse_sum * (1.0 / 1024.0)
+    def small_copy(k, over):
+        mine, size, buf, send, recv = (
+            (d, 8, sm_dp, smd_send, smd_recv) if over == 'dp' else (z, 4, sm_tp, smt_send, smt_recv))
+        peer = (mine + k) % size
+        return pltpu.make_async_remote_copy(
+            src_ref=buf.at[mine], dst_ref=buf.at[mine], send_sem=send.at[k], recv_sem=recv.at[mine],
+            device_id={over: peer})
+
+    def small_wait(k, over):
+        mine, size, buf, send, recv = (
+            (d, 8, sm_dp, smd_send, smd_recv) if over == 'dp' else (z, 4, sm_tp, smt_send, smt_recv))
+        peer = (mine + k) % size
+        pltpu.make_async_remote_copy(
+            src_ref=buf.at[peer], dst_ref=buf.at[peer], send_sem=send.at[k], recv_sem=recv.at[peer],
+            device_id={over: peer}).wait_recv()
+
+    def small_dp():
+        kl_tile = lax.fori_loop(0, TOK // 8, wsum, jnp.zeros((8, 128), F32))
+        loss = jnp.sum(kl_tile) + lse_sum
+        dw_row = jnp.sum(jnp.transpose(dw_acc[...]), axis=0, keepdims=True)
+        sm_dp[d] = jnp.concatenate([dw_row, jnp.full((1, D), loss, F32), jnp.zeros((6, D), F32)], axis=0)
+        for k in range(1, 8):
+            small_copy(k, 'dp').start()
+
+    def small_tp():
+        for k in range(1, 8):
+            small_wait(k, 'dp')
+        sm_tp[z] = tree(jnp.add, [sm_dp[k] for k in range(8)])
+        for k in range(1, 4):
+            small_copy(k, 'tp').start()
+
+    def small_end():
+        for k in range(1, 4):
+            small_wait(k, 'tp')
+        small_ref[...] = tree(jnp.add, [sm_tp[k] for k in range(4)])
+
+    def ticks(lo, hi):
+        def body(t, carry):
+            tick(t)
+            return carry
+        lax.fori_loop(lo, hi, body, 0)
+
+    stage1(NCH - 2, pp0)
+    stage1(NCH - 1, pp1)
+    t0 = npair
+    ticks(t0, t0 + 2)
+    slot(0)
+    ticks(t0 + 2, t0 + 3)
+    slot(1)
+    ticks(t0 + 3, t0 + 4)
+    slot(2)
+    ticks(t0 + 4, t0 + 6)
+    slot(3)
+    ticks(t0 + 6, t0 + 7)
+    slot(4)
+    ticks(t0 + 7, t0 + 8)
+    slot(5)
+    ticks(t0 + 8, t0 + 10)
+    slot(6)
+    small_dp()
+    ticks(t0 + 10, t0 + 11)
+    slot(7)
+    ticks(t0 + 11, NCH - 1)
+    slot(8)
+    small_tp()
+    stage3(NCH - 2)
+    stage4(NCH - 4)
+    stage3(NCH - 1)
+    stage4(NCH - 3)
+    slot(9)
+    dh_ref[...] = dh_f[...].astype(BF16)
+    stage4(NCH - 2)
+    stage4(NCH - 1)
+    small_end()
 
     for k in range(1, 4):
         st_copy(k).wait_send()
@@ -419,7 +501,15 @@
         for cp in s2_copies(c) + s3_copies(c):
             cp.wait_send()
 
-    loop(0, NCH, drain)
+    def drain_body(c, carry):
+        drain(c)
+        return carry
+
+    lax.fori_loop(0, NCH, drain_body, 0)
+    for k in range(1, 8):
+        small_copy(k, 'dp').wait_send()
+    for k in range(1, 4):
+        small_copy(k, 'tp').wait_send()
     for h in range(2):
         pos = where_of(h)[0]
         for b in range(4):
@@ -441,11 +531,10 @@
         out_shape=(
             jax.ShapeDtypeStruct((GRP, VLOC), F32),
             jax.ShapeDtypeStruct((D, TOK), BF16),
-            jax.ShapeDtypeStruct((D, 128), F32),
-            jax.ShapeDtypeStruct((8, 128), F32),
+            jax.ShapeDtypeStruct((8, D), F32),
         ),
         in_specs=[hbm] * 3 + [vmem] * 5,
-        out_specs=(vmem,) * 4,
+        out_specs=(vmem,) * 3,
         scratch_shapes=[
             pltpu.VMEM((3, TOK, CW), F32),
             pltpu.VMEM((3, TOK, CW), BF16),
@@ -465,10 +554,14 @@
             pltpu.VMEM((4, 8, TOK), F32),
             pltpu.VMEM((8, 8, 128), F32),
             pltpu.VMEM((8, 128), F32),
+            pltpu.VMEM((D, 128), F32),
+            pltpu.VMEM((8, 8, D), F32),
+            pltpu.VMEM((4, 8, D), F32),
         ] + [pltpu.VMEM((TOK, 128), F32)] * 5 + [
             dma((3, 4)), dma((4,)), dma((4,)), dma((8,)), dma((8,)),
             dma((NCH,)), dma((NCH,)), dma((2, NCH)), dma((2, NCH)), dma((2, NCH)), dma((2, NCH)),
             dma((8,)), dma((8,)), dma((8,)), dma((8,)),
+            dma((8,)), dma((8,)), dma((4,)), dma((4,)),
         ],
         compiler_params=pltpu.CompilerParams(
             collective_id=0, has_side_effects=True, vmem_limit_bytes=67_000_000),
@@ -484,9 +577,7 @@
         w_col = norm_w.astype(F32).reshape(D, 1)
         mask_row = mask_loc.astype(F32).reshape(1, TOK)
         th, g_t, stats = first_pass(hid_t, w_col, emb_t, teach_loc)
-        de_t, dh_t, dw_part, loss_part = second_pass(th, teach_loc, emb_t, g_t, hid_t, w_col, stats, mask_row)
-        packed = jnp.concatenate([jnp.sum(dw_part, axis=1), jnp.sum(loss_part).reshape(1)])
-        total = lax.psum(packed, ('tp', 'dp'))
-        return total[D], dh_t.T, de_t.T, total[:D]
+        de_t, dh_t, small = second_pass(th, teach_loc, emb_t, g_t, hid_t, w_col, stats, mask_row)
+        return small[1, 0], dh_t.T, de_t.T, small[0]
 
     return jax.shard_map(device_fn, mesh=mesh, in_specs=(P('dp', None), P(None), P('tp', None), P('dp', 'tp'), P('dp')), out_specs=(P(), P('dp', None), P('tp', 'dp'), P(None)), check_vma=False)

time: 299 us -> 212 us (0.71)
  blocking collectives: 42.9 us -> 0 us
  Pallas kernels: 239 us -> 197 us
  other arithmetic: 4.42 us -> 1.28 us
    psum x1 -> x0, blocking collectives: 42.9 us -> none  [device_fn(): total = lax.psum(packed, ('tp', 'dp'))]
    pallas_call x1, Pallas kernels: 192 us -> 149 us  [second_pass(): pl.pallas_call(grad_kernel, out_shape=(jax.ShapeDtypeStruct((GRP, VLOC),...]
    unnamed x12 -> x10, local copies, waits for them, and re-layouts: 9.28 us -> 9.27 us
where the time goes in v2:
time: 212 us; the launch traced here: 211 us
  Pallas kernels  197 us (93%)
  local copies, waits for them, and re-layouts  12.6 us (6%)
    pallas_call x1, Pallas kernels, second_pass(): pl.pallas_call(grad_kernel, out_shape=(jax.ShapeDtypeStruct((GRP, VLOC),...  149 us
    pallas_call x1, Pallas kernels, first_pass(): pl.pallas_call(stats_kernel, grid=(NCHA,), out_shape=(jax.ShapeDtypeStruc...  47.1 us
    unnamed x10, local copies, waits for them, and re-layouts  9.27 us

profile of v2, /device:TPU:0, one launch (start us, length us, event | category | flops | bytes accessed | tf_op | source)
XLA Modules:
  0.0 211.1 jit_solution(7916412887713152370)
XLA Ops:
  0.6 1.3 convert_element_type.4
  1.9 0.8 reshape.21.w_ref
  2.7 0.0 copy-start.1
  2.7 1.3 copy-done.1
  4.0 0.0 copy-start
  4.0 47.1 %shard_map.84 = (f32[1024,12288]{1,0:T(8,128)}, bf16[576,1024]{1,0:T(8,128)(2,1)S(1)}, f32[8,1024]{1,0:T(8,128)S(1)}) custom-call(bf16[576,1024]{1,0:T(8,128)(2,1)S(1)} %bitcast.7, f32[576,1]{1,0:T(8,128)S(1)} %reshape.21.w_ref, bf16[576,12288]{1,0:T(8,128)(2,1)} %bitcast.11, bf16[1024,12288]{1,0:T(8,128)(2,1)} %tea_hbm.1), custom_call_target="tpu_custom_call" | custom-call | flops 14495514624 | bytes 90000000 | tf_op jit(solution)/shard_map/pallas_call | solution.py:77
  51.2 0.0 copy-done
  51.2 0.0 copy-start.2
  51.2 1.0 copy-done.2
  52.2 0.0 copy-start.3
  52.2 0.6 copy-done.3
  52.8 149.4 %shard_map.85 = (f32[72,12288]{1,0:T(8,128)}, bf16[576,1024]{1,0:T(8,128)(2,1)}, f32[8,576]{1,0:T(8,128)}) custom-call(f32[1024,12288]{1,0:T(8,128)} %get-tuple-element.10.th_hbm, bf16[1024,12288]{1,0:T(8,128)(2,1)} %tea_hbm.1, bf16[576,12288]{1,0:T(8,128)(2,1)} %bitcast.12, bf16[576,1024]{1,0:T(8,128)(2,1)} %copy-done.2, bf16[576,1024]{1,0:T(8,128)(2,1)} %bitcast.6, ...), custom_call_target="tpu_custom_call" | custom-call | flops 28991029248 | bytes 100000000 | tf_op jit(solution)/shard_map/pallas_call | solution.py:529
  202.2 1.2 slice.6
  203.4 1.3 slice_reduce_fusion
  204.7 2.4 %copy.13 = bf16[1024,576]{0,1:T(8,128)(2,1)} copy(bf16[1024,576]{0,1:T(8,128)(2,1)} %bitcast.9) | data formatting | bytes 2359296
  207.1 4.0 %copy.14 = f32[12288,72]{0,1:T(8,128)} copy(f32[12288,72]{0,1:T(8,128)} %bitcast.8) | data formatting | bytes 7077888
Async XLA Ops:
  2.7 1.3 copy-start.1
  4.0 47.2 %copy-start = (f32[576,1]{1,0:T(8,128)}, f32[576,1]{1,0:T(8,128)S(1)}, u32[]{:S(2)}) copy-start(f32[576,1]{1,0:T(8,128)S(1)} %reshape.21.w_ref) | copy-start | bytes 6916
  51.2 1.0 copy-start.2
  52.2 0.6 copy-start.3

commit v3 on v2

--- a/solution.py
+++ b/solution.py
@@ -17,9 +17,9 @@
 CW = 512
 HALF = CW // 2
 NCH = VLOC // CW
-CWA = 512
-NCHA = VLOC // CWA
 RG = 32
+TB1 = 128
+TB2 = 512
 F32 = jnp.float32
 BF16 = jnp.bfloat16
 NT = (((1,), (1,)), ((), ()))
@@ -35,75 +35,10 @@
     return parts[0]
 
 
-def stats_kernel(hid_ref, w_ref, emb_ref, tea_ref, th_ref, gt_ref, st_ref, g_scr, s_acc, m_acc, t_acc):
-    step = pl.program_id(0)
-
-    @pl.when(step == 0)
-    def _():
-        x = hid_ref[...].astype(F32)
-        inv = lax.rsqrt(jnp.mean(x * x, axis=0, keepdims=True) + NORM_EPS)
-        gn = x * inv * (1.0 + w_ref[...])
-        gt_ref[...] = gn.astype(BF16)
-        g_scr[...] = jnp.transpose(gn).astype(BF16)
-        s_acc[...] = jnp.zeros_like(s_acc)
-        t_acc[...] = jnp.zeros_like(t_acc)
-        m_acc[...] = jnp.full_like(m_acc, -jnp.inf)
-
-    tb = 256
-    for blk in range(TOK // tb):
-        raw = jnp.dot(g_scr[blk * tb:(blk + 1) * tb, :], emb_ref[...], preferred_element_type=F32)
-        for sub in range(tb // RG):
-            rows = slice(blk * tb + sub * RG, blk * tb + (sub + 1) * RG)
-            th = jnp.tanh(raw[sub * RG:(sub + 1) * RG, :] * (1.0 / SOFT_CAP))
-            th_ref[rows, :] = th
-            s_acc[rows, :] += tree(jnp.add, lane_tiles(jnp.exp2(th * CAP2 - CAP2)))
-            tea = lane_tiles(tea_ref[rows, :].astype(F32))
-            old = m_acc[rows, :]
-            new = jnp.maximum(old, tree(jnp.maximum, tea))
-            m_acc[rows, :] = new
-            t_acc[rows, :] = t_acc[rows, :] * jnp.exp2((old - new) * LOG2E) + tree(
-                jnp.add, [jnp.exp2((part - new) * LOG2E) for part in tea])
-
-    @pl.when(step == NCHA - 1)
-    def _():
-        s_row = jnp.sum(jnp.transpose(s_acc[...]), axis=0, keepdims=True)
-        m_t = jnp.transpose(m_acc[...])
-        m_row = jnp.max(m_t, axis=0, keepdims=True)
-        t_row = jnp.sum(jnp.transpose(t_acc[...]) * jnp.exp2((m_t - m_row) * LOG2E), axis=0, keepdims=True)
-        st_ref[...] = jnp.concatenate([s_row, m_row, t_row, jnp.zeros((5, TOK), F32)], axis=0)
-
-
-def first_pass(hid_t, w_col, emb_t, teach):
-    return pl.pallas_call(
-        stats_kernel,
-        grid=(NCHA,),
-        out_shape=(
-            jax.ShapeDtypeStruct((TOK, VLOC), F32),
-            jax.ShapeDtypeStruct((D, TOK), BF16),
-            jax.ShapeDtypeStruct((8, TOK), F32),
-        ),
-        in_specs=[
-            pl.BlockSpec((D, TOK), lambda i: (0, 0)),
-            pl.BlockSpec((D, 1), lambda i: (0, 0)),
-            pl.BlockSpec((D, CWA), lambda i: (0, i)),
-            pl.BlockSpec((TOK, CWA), lambda i: (0, i)),
-        ],
-        out_specs=(
-            pl.BlockSpec((TOK, CWA), lambda i: (0, i)),
-            pl.BlockSpec((D, TOK), lambda i: (0, 0)),
-            pl.BlockSpec((8, TOK), lambda i: (0, 0)),
-        ),
-        scratch_shapes=[pltpu.VMEM((TOK, D), BF16)] + [pltpu.VMEM((TOK, 128), F32)] * 3,
-        compiler_params=pltpu.CompilerParams(
-            dimension_semantics=("arbitrary",), vmem_limit_bytes=48 * 1024 * 1024),
-        cost_estimate=pl.CostEstimate(
-            flops=2 * TOK * VLOC * D, bytes_accessed=90_000_000, transcendentals=3 * TOK * VLOC),
-    )(hid_t, w_col, emb_t, teach)
-
-
-def grad_kernel(th_hbm, tea_hbm, emb_hbm, gt_ref, hid_ref, w_ref, st_ref, mask_ref,
-                de_ref, dh_ref, small_ref,
-                th_buf, tea_buf, emb_buf, dr0, dr1, pp0, pp1, r1, r2a, r2b, r3a, r3b,
+def grad_kernel(tea_hbm, emb_hbm, hid_ref, w_ref, mask_ref,
+                th_hbm, de_ref, dh_ref, small_ref,
+                g_scr, gt_ref, st_ref, out_sem,
+                th_buf, tea_buf, emb_buf, dr, pp0, pp1, r1, r2a, r2b, r3a, r3b,
                 dg_ref, ar_in, dh_f, st_in, cnt_in, cnt_own, dw_acc, sm_dp, sm_tp, wgt, l2s, mtx, l2t, kl_acc,
                 in_sem, st_send, st_recv, cnt_send, cnt_recv,
                 s1_send, s1_recv, s2_send, s2_recv, s3_send, s3_recv,
@@ -120,26 +55,96 @@
     def fetch(i):
         cols = pl.ds(pl.multiple_of(i * CW, CW), CW)
         three = i % 3
-        four = i % 4
         return (
             pltpu.make_async_copy(th_hbm.at[:, cols], th_buf.at[three], in_sem.at[0, three]),
             pltpu.make_async_copy(tea_hbm.at[:, cols], tea_buf.at[three], in_sem.at[1, three]),
-            pltpu.make_async_copy(emb_hbm.at[:, cols], emb_buf.at[four], in_sem.at[2, four]),
+            pltpu.make_async_copy(emb_hbm.at[:, cols], emb_buf.at[three], in_sem.at[2, three]),
         )
 
     def start_fetch(i):
         for cp in fetch(i):
             cp.start()
 
-    start_fetch(0)
-    start_fetch(1)
+    def fetch_tea(i):
+        cols = pl.ds(pl.multiple_of(i * CW, CW), CW)
+        three = i % 3
+        return (
+            pltpu.make_async_copy(tea_hbm.at[:, cols], tea_buf.at[three], in_sem.at[1, three]),
+            pltpu.make_async_copy(emb_hbm.at[:, cols], emb_buf.at[three], in_sem.at[2, three]),
+        )
+
+    def put_th(i):
+        cols = pl.ds(pl.multiple_of(i * CW, CW), CW)
+        three = i % 3
+        return pltpu.make_async_copy(th_buf.at[three], th_hbm.at[:, cols], out_sem.at[three])
+
+    for k in range(2):
+        for cp in fetch_tea(k):
+            cp.start()
 
     barrier = pltpu.get_barrier_semaphore()
     for k in range(1, 4):
         pl.semaphore_signal(barrier, inc=1, device_id={'tp': (z + k) % 4})
     for k in range(1, 8):
         pl.semaphore_signal(barrier, inc=1, device_id={'dp': (d + k) % 8})
-    cnt_own[...] = jnp.full((8, 128), jnp.sum(mask_ref[...]), F32)
+
+    x_all = hid_ref[...].astype(F32)
+    g_all = x_all * lax.rsqrt(jnp.mean(x_all * x_all, axis=0, keepdims=True) + NORM_EPS) * (1.0 + w_ref[...])
+    gt_ref[...] = g_all.astype(BF16)
+    g_scr[...] = jnp.transpose(g_all).astype(BF16)
+    s_acc, m_acc, t_acc = wgt, l2s, mtx
+    s_acc[...] = jnp.zeros_like(s_acc)
+    t_acc[...] = jnp.zeros_like(t_acc)
+    m_acc[...] = jnp.full_like(m_acc, -jnp.inf)
+    cnt_own[...] = jnp.full((8, 128), jnp.sum(mask_ref[...].astype(F32)), F32)
+    dg_ref[...] = jnp.zeros_like(dg_ref)
+    kl_acc[...] = jnp.zeros_like(kl_acc)
+    dw_acc[...] = jnp.zeros_like(dw_acc)
+
+    def sums(i, three):
+        for cp in fetch_tea(i):
+            cp.wait()
+
+        @pl.when(i + 2 < NCH)
+        def _():
+            for cp in fetch_tea(i + 2):
+                cp.start()
+
+        @pl.when(i >= 3)
+        def _():
+            put_th(i - 3).wait()
+
+        tb = TB1
+        for blk in range(TOK // tb):
+            raw = jnp.dot(g_scr[blk * tb:(blk + 1) * tb, :], emb_buf[three], preferred_element_type=F32)
+            for sub in range(tb // RG):
+                rows = slice(blk * tb + sub * RG, blk * tb + (sub + 1) * RG)
+                th = jnp.tanh(raw[sub * RG:(sub + 1) * RG, :] * (1.0 / SOFT_CAP))
+                th_buf[three, rows, :] = th
+                s_acc[rows, :] += tree(jnp.add, lane_tiles(jnp.exp2(th * CAP2 - CAP2)))
+                tea = lane_tiles(tea_buf[three, rows, :].astype(F32))
+                old = m_acc[rows, :]
+                new = jnp.maximum(old, tree(jnp.maximum, tea))
+                m_acc[rows, :] = new
+                t_acc[rows, :] = t_acc[rows, :] * jnp.exp2((old - new) * LOG2E) + tree(
+                    jnp.add, [jnp.exp2((part - new) * LOG2E) for part in tea])
+        put_th(i).start()
+
+    def sums3(t, carry):
+        for three in range(3):
+            sums(3 * t + three, three)
+        return carry
+
+    lax.fori_loop(0, NCH // 3, sums3, 0)
+    for k in range(3):
+        put_th(NCH - 3 + k).wait()
+    start_fetch(0)
+    start_fetch(1)
+    s_row = jnp.sum(jnp.transpose(s_acc[...]), axis=0, keepdims=True)
+    m_t = jnp.transpose(m_acc[...])
+    m_row = jnp.max(m_t, axis=0, keepdims=True)
+    t_row = jnp.sum(jnp.transpose(t_acc[...]) * jnp.exp2((m_t - m_row) * LOG2E), axis=0, keepdims=True)
+    st_ref[...] = jnp.concatenate([s_row, m_row, t_row, jnp.zeros((5, TOK), F32)], axis=0)
     pl.semaphore_wait(barrier, 10)
 
     def st_copy(k):
@@ -156,9 +161,6 @@
         st_copy(k).start()
     for k in range(1, 8):
         cnt_copy(k).start()
-    dg_ref[...] = jnp.zeros_like(dg_ref)
-    kl_acc[...] = jnp.zeros_like(kl_acc)
-    dw_acc[...] = jnp.zeros_like(dw_acc)
     for k in range(1, 4):
         st_copy(k).wait_recv()
     for k in range(1, 8):
@@ -171,7 +173,7 @@
     count = cnt_own[0:1, :]
     for k in range(1, 8):
         count = count + cnt_in[k][0:1, :]
-    w_row = mask_ref[...] / jnp.concatenate([count] * (TOK // 128), axis=1)
+    w_row = mask_ref[...].astype(F32) / jnp.concatenate([count] * (TOK // 128), axis=1)
     l2s_row = jnp.log2(s_tot) + CAP2
     l2t_row = jnp.log2(t_tot)
 
@@ -201,14 +203,24 @@
                 dr_ref[rows, cols] = ((p_s - p_t) * w_b * (1.0 - th * th)).astype(BF16)
             kl_acc[rows, :] += tree(jnp.add, kl)
 
-    def emb_piece(dr_ref, pp_ref, k):
-        part = jnp.dot(gt_ref[...], dr_ref[:, k * HALF:(k + 1) * HALF], preferred_element_type=F32)
-        for grp in range(8):
-            pp_ref[grp % 2, grp // 4, (grp // 2) % 2, :, k * HALF:(k + 1) * HALF] = part[grp * GRP:(grp + 1) * GRP, :]
-
-    def hid_piece(i, dr_ref, k):
-        cols = slice(k * 256, (k + 1) * 256)
-        dg_ref[:, cols] += lax.dot_general(emb_buf[i % 4], dr_ref[cols, :], NT, preferred_element_type=F32)
+    def products(i, pp_ref, k):
+        rows = slice(k * TB2, (k + 1) * TB2)
+        for col in range(rows.start, rows.stop, 256):
+            cols = slice(col, col + 256)
+            dg_ref[:, cols] += lax.dot_general(emb_buf[i % 3], dr[cols, :], NT, preferred_element_type=F32)
+        for half in range(2):
+            cols = slice(half * HALF, (half + 1) * HALF)
+            part = jnp.dot(gt_ref[:, rows], dr[rows, cols], preferred_element_type=F32)
+            for grp in range(8):
+                at = (grp % 2, grp // 4, (grp // 2) % 2, slice(None), cols)
+                piece = part[grp * GRP:(grp + 1) * GRP, :]
+                pp_ref[at] = piece if k == 0 else pp_ref[at] + piece
+
+    def whole(i, pp_ref):
+        n = TOK // TB2
+        for k in range(n):
+            elementwise(i, dr, nsub * k // n, nsub * (k + 1) // n)
+            products(i, pp_ref, k)
 
     def s1_copy(c, pp_ref):
         return pltpu.make_async_remote_copy(
@@ -269,46 +281,38 @@
         for cp in fetch(i):
             cp.wait()
 
-    def both(i, dr_new, dr_old, pp_ref, cuts=6):
-        for k in range(cuts):
-            if k < 2:
-                emb_piece(dr_old, pp_ref, k)
-            else:
-                hid_piece(i - 1, dr_old, k - 2)
-            elementwise(i, dr_new, nsub * k // cuts, nsub * (k + 1) // cuts)
+    def tick(t):
+        stage2(t + 2)
+
+        @pl.when(t >= 1)
+        def _():
+            stage3(t - 1)
+
+        @pl.when(t >= 4)
+        def _():
+            stage4(t - 4)
 
     wait_in(0)
     start_fetch(2)
-    elementwise(0, dr0, 0, nsub)
-    wait_in(1)
-    start_fetch(3)
-    both(1, dr1, dr0, pp0)
+    whole(0, pp0)
     s1_copy(0, pp0).start()
 
-    def tick(t):
-        stage2(t + 1)
-        stage3(t - 1)
-
-        @pl.when(t >= 3)
-        def _():
-            stage4(t - 3)
-
     def pair(t, carry):
-        for par, (dr_new, dr_old, pp_new, pp_old) in enumerate(((dr0, dr1, pp1, pp0), (dr1, dr0, pp0, pp1))):
-            i = 2 + 2 * t + par
+        for par, (pp_new, pp_old) in enumerate(((pp1, pp0), (pp0, pp1))):
+            i = 1 + 2 * t + par
             wait_in(i)
 
             @pl.when(i + 2 < NCH)
             def _():
                 start_fetch(i + 2)
 
-            @pl.when(i >= 3)
+            @pl.when(i >= 2)
             def _():
-                s1_copy(i - 3, pp_new).wait_send()
-
-            both(i, dr_new, dr_old, pp_new)
-            s1_copy(i - 1, pp_new).start()
-            stage1(i - 2, pp_old)
+                s1_copy(i - 2, pp_new).wait_send()
+
+            whole(i, pp_new)
+            s1_copy(i, pp_new).start()
+            stage1(i - 1, pp_old)
             if par == 0:
                 @pl.when(t == 0)
                 def _():
@@ -316,7 +320,7 @@
 
                 @pl.when(t > 0)
                 def _():
-                    tick(t)
+                    tick(t - 1)
             else:
                 @pl.when(t == 0)
                 def _():
@@ -325,12 +329,12 @@
 
     npair = (NCH - 2) // 2
     lax.fori_loop(0, npair, pair, 0)
+    wait_in(NCH - 1)
     s1_copy(NCH - 3, pp1).wait_send()
-    for k in range(2):
-        emb_piece(dr1, pp1, k)
+    whole(NCH - 1, pp1)
     s1_copy(NCH - 1, pp1).start()
-    for k in range(4):
-        hid_piece(NCH - 1, dr1, k)
+    stage1(NCH - 2, pp0)
+    tick(npair - 1)
 
     def where_of(h):
         pos = z if h == 0 else 3 - z
@@ -457,35 +461,24 @@
             return carry
         lax.fori_loop(lo, hi, body, 0)
 
-    stage1(NCH - 2, pp0)
     stage1(NCH - 1, pp1)
     t0 = npair
-    ticks(t0, t0 + 2)
-    slot(0)
-    ticks(t0 + 2, t0 + 3)
-    slot(1)
-    ticks(t0 + 3, t0 + 4)
-    slot(2)
-    ticks(t0 + 4, t0 + 6)
-    slot(3)
-    ticks(t0 + 6, t0 + 7)
-    slot(4)
-    ticks(t0 + 7, t0 + 8)
-    slot(5)
-    ticks(t0 + 8, t0 + 10)
-    slot(6)
-    small_dp()
-    ticks(t0 + 10, t0 + 11)
-    slot(7)
-    ticks(t0 + 11, NCH - 1)
+    for n, cuts in enumerate((0, 1, 2, 4, 5, 7, 8, 10)):
+        ticks(t0 + cuts, t0 + (1, 2, 4, 5, 7, 8, 10, NCH - 2 - t0)[n])
+        slot(n)
+        if n == 6:
+            small_dp()
+    stage3(NCH - 3)
+    stage4(NCH - 6)
     slot(8)
+    stage3(NCH - 2)
+    stage4(NCH - 5)
     small_tp()
-    stage3(NCH - 2)
+    stage3(NCH - 1)
     stage4(NCH - 4)
-    stage3(NCH - 1)
-    stage4(NCH - 3)
     slot(9)
     dh_ref[...] = dh_f[...].astype(BF16)
+    stage4(NCH - 3)
     stage4(NCH - 2)
     stage4(NCH - 1)
     small_end()
@@ -522,24 +515,28 @@
                 bc_copy(h, b).wait_send()
 
 
-def second_pass(th, teach, emb_t, g_t, hid_t, w_col, stats, mask_row):
+def one_pass(teach, emb_t, hid_t, w_col, mask_row):
     vmem = pl.BlockSpec(memory_space=pltpu.VMEM)
     hbm = pl.BlockSpec(memory_space=pl.ANY)
     dma = pltpu.SemaphoreType.DMA
     return pl.pallas_call(
         grad_kernel,
         out_shape=(
+            jax.ShapeDtypeStruct((TOK, VLOC), F32),
             jax.ShapeDtypeStruct((GRP, VLOC), F32),
             jax.ShapeDtypeStruct((D, TOK), BF16),
             jax.ShapeDtypeStruct((8, D), F32),
         ),
-        in_specs=[hbm] * 3 + [vmem] * 5,
-        out_specs=(vmem,) * 3,
+        in_specs=[hbm] * 2 + [vmem] * 3,
+        out_specs=(hbm,) + (vmem,) * 3,
         scratch_shapes=[
+            pltpu.VMEM((TOK, D), BF16),
+            pltpu.VMEM((D, TOK), BF16),
+            pltpu.VMEM((8, TOK), F32),
+            dma((3,)),
             pltpu.VMEM((3, TOK, CW), F32),
             pltpu.VMEM((3, TOK, CW), BF16),
-            pltpu.VMEM((4, D, CW), BF16),
-            pltpu.VMEM((TOK, CW), BF16),
+            pltpu.VMEM((3, D, CW), BF16),
             pltpu.VMEM((TOK, CW), BF16),
             pltpu.VMEM((2, 2, 2, GRP, CW), F32),
             pltpu.VMEM((2, 2, 2, GRP, CW), F32),
@@ -558,7 +555,7 @@
             pltpu.VMEM((8, 8, D), F32),
             pltpu.VMEM((4, 8, D), F32),
         ] + [pltpu.VMEM((TOK, 128), F32)] * 5 + [
-            dma((3, 4)), dma((4,)), dma((4,)), dma((8,)), dma((8,)),
+            dma((3, 3)), dma((4,)), dma((4,)), dma((8,)), dma((8,)),
             dma((NCH,)), dma((NCH,)), dma((2, NCH)), dma((2, NCH)), dma((2, NCH)), dma((2, NCH)),
             dma((8,)), dma((8,)), dma((8,)), dma((8,)),
             dma((8,)), dma((8,)), dma((4,)), dma((4,)),
@@ -566,8 +563,8 @@
         compiler_params=pltpu.CompilerParams(
             collective_id=0, has_side_effects=True, vmem_limit_bytes=67_000_000),
         cost_estimate=pl.CostEstimate(
-            flops=4 * TOK * VLOC * D, bytes_accessed=100_000_000, transcendentals=2 * TOK * VLOC),
-    )(th, teach, emb_t, g_t, hid_t, w_col, stats, mask_row)
+            flops=6 * TOK * VLOC * D, bytes_accessed=190_000_000, transcendentals=5 * TOK * VLOC),
+    )(teach, emb_t, hid_t, w_col, mask_row)
 
 
 def solution(mesh):
@@ -575,9 +572,8 @@
         hid_t = hid_loc.T
         emb_t = emb_loc.T
         w_col = norm_w.astype(F32).reshape(D, 1)
-        mask_row = mask_loc.astype(F32).reshape(1, TOK)
-        th, g_t, stats = first_pass(hid_t, w_col, emb_t, teach_loc)
-        de_t, dh_t, small = second_pass(th, teach_loc, emb_t, g_t, hid_t, w_col, stats, mask_row)
+        mask_row = mask_loc.reshape(1, TOK)
+        _, de_t, dh_t, small = one_pass(teach_loc, emb_t, hid_t, w_col, mask_row)
         return small[1, 0], dh_t.T, de_t.T, small[0]
 
     return jax.shard_map(device_fn, mesh=mesh, in_specs=(P('dp', None), P(None), P('tp', None), P('dp', 'tp'), P('dp')), out_specs=(P(), P('dp', None), P('tp', 'dp'), P(None)), check_vma=False)

time: 212 us -> 194 us (0.915)
  Pallas kernels: 197 us -> 183 us
    pallas_call x2 -> x1, Pallas kernels: 197 us -> 183 us  [one_pass(): pl.pallas_call(grad_kernel, out_shape=(jax.ShapeDtypeStruct((TOK, VLOC),...]
    unnamed x10 -> x2, local copies, waits for them, and re-layouts: 9.27 us -> 6.38 us
where the time goes in v3:
time: 194 us
  Pallas kernels  183 us (94%)
  local copies, waits for them, and re-layouts  10.5 us (5%)
    pallas_call x1, Pallas kernels, one_pass(): pl.pallas_call(grad_kernel, out_shape=(jax.ShapeDtypeStruct((TOK, VLOC),...  183 us
    unnamed x2, local copies, waits for them, and re-layouts  6.38 us

profile of v3, /device:TPU:0, one launch (start us, length us, event | category | flops | bytes accessed | tf_op | source)
XLA Modules:
  0.0 194.1 jit_solution(4116812160036925385)
XLA Ops:
  0.6 1.5 reshape.21.w_ref
  2.2 183.1 %shard_map.84 = (f32[1024,12288]{1,0:T(8,128)}, f32[72,12288]{1,0:T(8,128)}, bf16[576,1024]{1,0:T(8,128)(2,1)}, f32[8,576]{1,0:T(8,128)}) custom-call(bf16[1024,12288]{1,0:T(8,128)(2,1)} %tea_hbm.1, bf16[576,12288]{1,0:T(8,128)(2,1)} %bitcast.8, bf16[576,1024]{1,0:T(8,128)(2,1)} %bitcast.9, f32[576,1]{1,0:T(8,128)} %reshape.21.w_ref, s32[1,1024]{1,0:T(1,128)} %bitcast.10), custom_call_target="tpu_custom_call" | custom-call | flops 43486543872 | bytes 190000000 | tf_op jit(solution)/shard_map/pallas_call | solution.py:522
  185.2 1.2 slice.6
  186.4 1.3 slice_reduce_fusion
  187.8 2.4 %copy.12 = bf16[1024,576]{0,1:T(8,128)(2,1)} copy(bf16[1024,576]{0,1:T(8,128)(2,1)} %bitcast.7) | data formatting | bytes 2359296
  190.1 4.0 %copy.13 = f32[12288,72]{0,1:T(8,128)} copy(f32[12288,72]{0,1:T(8,128)} %bitcast.6) | data formatting | bytes 7077888

commit v4 on v3

--- a/solution.py
+++ b/solution.py
@@ -121,7 +121,7 @@
                 rows = slice(blk * tb + sub * RG, blk * tb + (sub + 1) * RG)
                 th = jnp.tanh(raw[sub * RG:(sub + 1) * RG, :] * (1.0 / SOFT_CAP))
                 th_buf[three, rows, :] = th
-                s_acc[rows, :] += tree(jnp.add, lane_tiles(jnp.exp2(th * CAP2 - CAP2)))
+                s_acc[rows, :] += tree(jnp.add, lane_tiles(jnp.exp2(th * CAP2)))
                 tea = lane_tiles(tea_buf[three, rows, :].astype(F32))
                 old = m_acc[rows, :]
                 new = jnp.maximum(old, tree(jnp.maximum, tea))
@@ -174,16 +174,16 @@
     for k in range(1, 8):
         count = count + cnt_in[k][0:1, :]
     w_row = mask_ref[...].astype(F32) / jnp.concatenate([count] * (TOK // 128), axis=1)
-    l2s_row = jnp.log2(s_tot) + CAP2
+    l2s_row = jnp.log2(s_tot)
     l2t_row = jnp.log2(t_tot)
 
     def to_rows(row):
         return jnp.transpose(jnp.broadcast_to(row, (128, TOK)))
 
-    wgt[...] = to_rows(w_row)
-    l2s[...] = to_rows(l2s_row)
+    l2w_row = jnp.log2(w_row)
+    l2s[...] = to_rows(l2s_row - l2w_row)
     mtx[...] = to_rows(m_tot)
-    l2t[...] = to_rows(l2t_row)
+    l2t[...] = to_rows(l2t_row - l2w_row)
     lse_part = w_row * ((l2s_row - l2t_row) * LN2 - m_tot)
     lse_sum = jnp.where(z == 0, jnp.sum(lse_part), 0.0)
 
@@ -191,7 +191,7 @@
         slot = i % 3
         for sub in range(lo, hi):
             rows = slice(sub * RG, (sub + 1) * RG)
-            w_b, ls_b, m_b, lt_b = wgt[rows, :], l2s[rows, :], mtx[rows, :], l2t[rows, :]
+            ls_b, m_b, lt_b = l2s[rows, :], mtx[rows, :], l2t[rows, :]
             kl = []
             for q in range(CW // 128):
                 cols = slice(q * 128, (q + 1) * 128)
@@ -200,7 +200,7 @@
                 p_s = jnp.exp2(th * CAP2 - ls_b)
                 p_t = jnp.exp2((tea - m_b) * LOG2E - lt_b)
                 kl.append(p_t * (tea - SOFT_CAP * th))
-                dr_ref[rows, cols] = ((p_s - p_t) * w_b * (1.0 - th * th)).astype(BF16)
+                dr_ref[rows, cols] = ((p_s - p_t) * (1.0 - th * th)).astype(BF16)
             kl_acc[rows, :] += tree(jnp.add, kl)
 
     def products(i, pp_ref, k):
@@ -346,42 +346,43 @@
         lo = h * 512 + b * 128
         return slice(lo, lo + 128)
 
-    def ar_first(h, b):
-        pos, up, _ = where_of(h)
+    def rows_of(r):
+        return pl.ds(r * (D // 2), D // 2)
+
+    def ar_copy(h, b, r, first=False):
+        _, up, _ = where_of(h)
         idx = 4 * h + b
+        dst = ar_in.at[idx, rows_of(r)]
+        src = dg_ref.at[rows_of(r), pl.ds(h * 512 + b * 128, 128)] if first else dst
         return pltpu.make_async_remote_copy(
-            src_ref=dg_ref.at[:, pl.ds(h * 512 + b * 128, 128)], dst_ref=ar_in.at[idx],
-            send_sem=ar_send.at[idx], recv_sem=ar_recv.at[idx], device_id={'tp': up})
-
-    def ar_next(h, b):
-        pos, up, _ = where_of(h)
-        idx = 4 * h + b
-        return pltpu.make_async_remote_copy(
-            src_ref=ar_in.at[idx], dst_ref=ar_in.at[idx],
-            send_sem=ar_send.at[idx], recv_sem=ar_recv.at[idx], device_id={'tp': up})
-
-    def bc_copy(h, b):
+            src_ref=src, dst_ref=dst,
+            send_sem=ar_send.at[2 * idx + r], recv_sem=ar_recv.at[2 * idx + r], device_id={'tp': up})
+
+    def bc_copy(h, b, r):
         _, _, down = where_of(h)
         idx = 4 * h + b
-        part = dh_f.at[:, pl.ds(h * 512 + b * 128, 128)]
+        part = dh_f.at[rows_of(r), pl.ds(h * 512 + b * 128, 128)]
         return pltpu.make_async_remote_copy(
             src_ref=part, dst_ref=part,
-            send_sem=bc_send.at[idx], recv_sem=bc_recv.at[idx], device_id={'tp': down})
+            send_sem=bc_send.at[2 * idx + r], recv_sem=bc_recv.at[2 * idx + r], device_id={'tp': down})
 
     for b in range(4):
         for h in range(2):
             @pl.when(where_of(h)[0] == 0)
             def _():
-                ar_first(h, b).start()
+                for r in range(2):
+                    ar_copy(h, b, r, first=True).start()
 
     def add_on(h, b):
         idx = 4 * h + b
-        ar_next(h, b).wait_recv()
-        ar_in[idx] += dg_ref[:, lanes(h, b)]
-        ar_next(h, b).start()
+        for r in range(2):
+            ar_copy(h, b, r).wait_recv()
+            ar_in[idx, rows_of(r)] += dg_ref[rows_of(r), lanes(h, b)]
+            ar_copy(h, b, r).start()
 
     def finish(h, b):
-        ar_next(h, b).wait_recv()
+        for r in range(2):
+            ar_copy(h, b, r).wait_recv()
         dg = ar_in[4 * h + b] + dg_ref[:, lanes(h, b)]
         x = hid_ref[:, lanes(h, b)].astype(F32)
         inv = lax.rsqrt(jnp.mean(x * x, axis=0, keepdims=True) + NORM_EPS)
@@ -389,12 +390,14 @@
         du = dg * (1.0 + w_ref[...])
         inner = jnp.sum(du * x, axis=0, keepdims=True)
         dh_f[:, lanes(h, b)] = du * inv - x * (inv * inv * inv * inner * (1.0 / D))
-        bc_copy(h, b).start()
+        for r in range(2):
+            bc_copy(h, b, r).start()
 
     def spread(h, b, pos):
-        bc_copy(h, b).wait_recv()
-        if pos > 0:
-            bc_copy(h, b).start()
+        for r in range(2):
+            bc_copy(h, b, r).wait_recv()
+            if pos > 0:
+                bc_copy(h, b, r).start()
 
     def slot(s):
         for pos in (1, 2, 3):
@@ -408,7 +411,7 @@
                         else:
                             finish(h, b)
         for pos in (2, 1, 0):
-            b = s - 4 - (2 - pos)
+            b = s - 3 - (2 - pos)
             if 0 <= b < 4:
                 for h in range(2):
                     @pl.when(where_of(h)[0] == pos)
@@ -417,7 +420,7 @@
 
     def wsum(k, carry):
         rows = pl.ds(pl.multiple_of(k * 8, 8), 8)
-        return carry + wgt[rows, :] * kl_acc[rows, :]
+        return carry + kl_acc[rows, :]
 
     def small_copy(k, over):
         mine, size, buf, send, recv = (
@@ -463,10 +466,11 @@
 
     stage1(NCH - 1, pp1)
     t0 = npair
-    for n, cuts in enumerate((0, 1, 2, 4, 5, 7, 8, 10)):
-        ticks(t0 + cuts, t0 + (1, 2, 4, 5, 7, 8, 10, NCH - 2 - t0)[n])
+    before = (0, 1, 2, 3, 5, 6, 8, 9, NCH - 2 - t0)
+    for n in range(8):
+        ticks(t0 + before[n], t0 + before[n + 1])
         slot(n)
-        if n == 6:
+        if n == 5:
             small_dp()
     stage3(NCH - 3)
     stage4(NCH - 6)
@@ -476,7 +480,6 @@
     small_tp()
     stage3(NCH - 1)
     stage4(NCH - 4)
-    slot(9)
     dh_ref[...] = dh_f[...].astype(BF16)
     stage4(NCH - 3)
     stage4(NCH - 2)
@@ -506,13 +509,14 @@
     for h in range(2):
         pos = where_of(h)[0]
         for b in range(4):
-            @pl.when(pos < 3)
-            def _():
-                ar_next(h, b).wait_send()
-
-            @pl.when(pos > 0)
-            def _():
-                bc_copy(h, b).wait_send()
+            for r in range(2):
+                @pl.when(pos < 3)
+                def _():
+                    ar_copy(h, b, r).wait_send()
+
+                @pl.when(pos > 0)
+                def _():
+                    bc_copy(h, b, r).wait_send()
 
 
 def one_pass(teach, emb_t, hid_t, w_col, mask_row):
@@ -557,7 +561,7 @@
         ] + [pltpu.VMEM((TOK, 128), F32)] * 5 + [
             dma((3, 3)), dma((4,)), dma((4,)), dma((8,)), dma((8,)),
             dma((NCH,)), dma((NCH,)), dma((2, NCH)), dma((2, NCH)), dma((2, NCH)), dma((2, NCH)),
-            dma((8,)), dma((8,)), dma((8,)), dma((8,)),
+            dma((16,)), dma((16,)), dma((16,)), dma((16,)),
             dma((8,)), dma((8,)), dma((4,)), dma((4,)),
         ],
         compiler_params=pltpu.CompilerParams(
@@ -567,6 +571,36 @@
     )(teach, emb_t, hid_t, w_col, mask_row)
 
 
+def out_kernel(de_in, dh_in, de_out, dh_out, de_buf, dh_buf, sem_in, sem_out):
+    n = 6
+    wide = VLOC // n
+    pieces = [(dh_in, dh_buf, dh_out)] + [
+        (de_in.at[:, pl.ds(k * wide, wide)], de_buf.at[k], de_out.at[:, pl.ds(k * wide, wide)]) for k in range(n)]
+    ins = [pltpu.make_async_copy(src, buf, sem_in.at[k]) for k, (src, buf, _) in enumerate(pieces)]
+    outs = [pltpu.make_async_copy(buf, dst, sem_out.at[k]) for k, (_, buf, dst) in enumerate(pieces)]
+    for cp in ins:
+        cp.start()
+    for arrive, leave in zip(ins, outs):
+        arrive.wait()
+        leave.start()
+    for cp in outs:
+        cp.wait()
+
+
+def hand_over(de_t, dh_t):
+    hbm = pl.BlockSpec(memory_space=pl.ANY)
+    return pl.pallas_call(
+        out_kernel,
+        out_shape=(jax.ShapeDtypeStruct((GRP, VLOC), F32), jax.ShapeDtypeStruct((D, TOK), BF16)),
+        in_specs=[hbm] * 2,
+        out_specs=(hbm,) * 2,
+        scratch_shapes=[
+            pltpu.VMEM((6, GRP, VLOC // 6), F32), pltpu.VMEM((D, TOK), BF16),
+            pltpu.SemaphoreType.DMA((7,)), pltpu.SemaphoreType.DMA((7,))],
+        compiler_params=pltpu.CompilerParams(vmem_limit_bytes=60 * 1024 * 1024),
+    )(de_t, dh_t)
+
+
 def solution(mesh):
     def device_fn(hid_loc, norm_w, emb_loc, teach_loc, mask_loc):
         hid_t = hid_loc.T
@@ -574,6 +608,7 @@
         w_col = norm_w.astype(F32).reshape(D, 1)
         mask_row = mask_loc.reshape(1, TOK)
         _, de_t, dh_t, small = one_pass(teach_loc, emb_t, hid_t, w_col, mask_row)
+        de_t, dh_t = hand_over(de_t, dh_t)
         return small[1, 0], dh_t.T, de_t.T, small[0]
 
     return jax.shard_map(device_fn, mesh=mesh, in_specs=(P('dp', None), P(None), P('tp', None), P('dp', 'tp'), P('dp')), out_specs=(P(), P('dp', None), P('tp', 'dp'), P(None)), check_vma=False)

time: 194 us -> 191 us (0.985)
  local copies, waits for them, and re-layouts: 10.5 us -> 4.07 us
  Pallas kernels: 183 us -> 186 us
    unnamed x2 -> x0, local copies, waits for them, and re-layouts: 6.38 us -> none
    pallas_call x0 -> x1, Pallas kernels: none -> 3.57 us  [hand_over(): pl.pallas_call(out_kernel, out_shape=(jax.ShapeDtypeStruct((GRP, VLOC), F...]
where the time goes in v4:
time: 191 us
  Pallas kernels  186 us (97%)
  local copies, waits for them, and re-layouts  4.07 us (2%)
    pallas_call x1, Pallas kernels, one_pass(): pl.pallas_call(grad_kernel, out_shape=(jax.ShapeDtypeStruct((TOK, VLOC),...  183 us

profile of v4, /device:TPU:0, one launch (start us, length us, event | category | flops | bytes accessed | tf_op | source)
XLA Modules:
  0.0 190.8 jit_solution(330575229018901568)
XLA Ops:
  0.6 1.5 reshape.21.w_ref
  2.2 182.5 %shard_map.84 = (f32[1024,12288]{1,0:T(8,128)}, f32[72,12288]{1,0:T(8,128)}, bf16[576,1024]{1,0:T(8,128)(2,1)}, f32[8,576]{1,0:T(8,128)}) custom-call(bf16[1024,12288]{1,0:T(8,128)(2,1)} %tea_hbm.1, bf16[576,12288]{1,0:T(8,128)(2,1)} %bitcast.6, bf16[576,1024]{1,0:T(8,128)(2,1)} %bitcast.8, f32[576,1]{1,0:T(8,128)} %reshape.21.w_ref, s32[1,1024]{1,0:T(1,128)} %bitcast.10), custom_call_target="tpu_custom_call" | custom-call | flops 43486543872 | bytes 190000000 | tf_op jit(solution)/shard_map/pallas_call | solution.py:526
  184.7 1.2 slice.6
  185.9 3.6 %shard_map.85 = (f32[72,12288]{1,0:T(8,128)}, bf16[576,1024]{1,0:T(8,128)(2,1)}) custom-call(f32[72,12288]{1,0:T(8,128)} %get-tuple-element.10.de_in, bf16[576,1024]{1,0:T(8,128)(2,1)} %get-tuple-element.11.dh_in), custom_call_target="tpu_custom_call" | custom-call | tf_op jit(solution)/shard_map/pallas_call | solution.py:592
  189.5 1.3 slice_reduce_fusion
